TPU v7x, 32 devices: a whole 2x2x4 slice. The times are simulated.
32 devices in a mesh: data: 4 (over x, y), model: 8 (over z, core).
Axes of the slice: x: 2, y: 2, z: 4, core: 2. Of those that a mesh axis runs over, the one named last changes fastest.
Arguments:
- resid_x: bfloat16 [16384, 2048], P('data'), parts along dimension 0
- ln_mean: float32 [16384], P('data'), parts along dimension 0
- ln_rstd: float32 [16384], P('data'), parts along dimension 0
- ln_gain: bfloat16 [2048], replicated
- grad_y: bfloat16 [16384, 2048], P('data'), parts along dimension 0
- w_qkv: bfloat16 [2048, 6144], P(None, 'model')
- w_out: bfloat16 [8, 256, 2048], P('model')
- w_up: bfloat16 [2048, 8192], P(None, 'model')
- w_down: bfloat16 [8192, 2048], P('model')
Outputs:
- output 1: bfloat16 [16384, 2048], P('data'), parts along dimension 0
- output 2: bfloat16 [8192, 6144], P('data', 'model'), parts along dimension 0
- output 3: bfloat16 [32, 256, 2048], P(('data', 'model')), parts along dimension 0
- output 4: bfloat16 [8192, 8192], P('data', 'model'), parts along dimension 0
- output 5: bfloat16 [32768, 2048], P(('data', 'model')), parts along dimension 0
There are 4 independent parts. A program takes and returns all parts, laid end to end along the dimension named above; an argument that names none is the same for every part.
All inputs are finite; a program needn't handle non-finite values.
Results may differ from a plain program's by a relative error of at most 0.0138052.
Values are sent between devices in bfloat16 or wider.
A program may use at most 1 GiB of HBM per device.

v0:
```python
import jax
import jax.numpy as jnp
from jax import lax
from jax.sharding import PartitionSpec as P

CONTRACT_ROWS = (((0,), (0,)), ((), ()))
CONTRACT_COLS = (((1,), (1,)), ((), ()))


def rope_tables(tokens, rot_dim):
    half_rot = rot_dim // 2
    positions = jnp.arange(tokens, dtype=jnp.float32)[:, None]
    inv_freq = jnp.power(10000.0, -2.0 * jnp.arange(half_rot, dtype=jnp.float32) / rot_dim)
    angles = positions * inv_freq[None, :]
    return jnp.cos(angles)[:, None, :], jnp.sin(angles)[:, None, :]


def rotate(vectors, rope_cos, rope_sin):
    half_rot = rope_cos.shape[-1]
    first_half = vectors[..., :half_rot]
    second_half = vectors[..., half_rot:2 * half_rot]
    return jnp.concatenate([first_half * rope_cos - second_half * rope_sin, second_half * rope_cos + first_half * rope_sin, vectors[..., 2 * half_rot:]], axis=-1)


def exact_gelu(pre_act):
    return jax.nn.gelu(pre_act, approximate=False)


def attention_pair(q_rot, k_rot, values, d_attn):
    tokens = q_rot.shape[-3]
    att_scale = q_rot.shape[-1] ** -0.5
    scores = jnp.einsum("...qhd,...khd->...hqk", q_rot, k_rot, preferred_element_type=jnp.float32) * att_scale
    causal = jnp.arange(tokens)[:, None] >= jnp.arange(tokens)[None, :]
    attn_probs = jax.nn.softmax(jnp.where(causal, scores, -1e30), axis=-1)
    probs_bf = attn_probs.astype(jnp.bfloat16)
    attn_out = jnp.einsum("...hqk,...khd->...qhd", probs_bf, values, preferred_element_type=jnp.float32).astype(jnp.bfloat16)
    d_probs = jnp.einsum("...qhd,...khd->...hqk", d_attn, values, preferred_element_type=jnp.float32)
    d_values = jnp.einsum("...hqk,...qhd->...khd", probs_bf, d_attn, preferred_element_type=jnp.float32)
    row_delta = jnp.sum(attn_probs * d_probs, axis=-1, keepdims=True)
    d_scores = (attn_probs * (d_probs - row_delta) * att_scale).astype(jnp.bfloat16)
    d_q_rot = jnp.einsum("...hqk,...khd->...qhd", d_scores, k_rot, preferred_element_type=jnp.float32)
    d_k_rot = jnp.einsum("...hqk,...qhd->...khd", d_scores, q_rot, preferred_element_type=jnp.float32)
    return attn_out, d_q_rot, d_k_rot, d_values


def ln_backward(d_normed, x_hat, gain_f32, ln_rstd, grad_y):
    d_hat = d_normed * gain_f32
    mean_d = jnp.mean(d_hat, axis=-1, keepdims=True)
    mean_dx = jnp.mean(d_hat * x_hat, axis=-1, keepdims=True)
    grad_in = ln_rstd[:, None] * (d_hat - mean_d - x_hat * mean_dx)
    return (grad_y.astype(jnp.float32) + grad_in).astype(jnp.bfloat16)


def solution(mesh):
    def device_step(resid_x, ln_mean, ln_rstd, ln_gain, grad_y, w_qkv, w_out, w_up, w_down):
        heads_local = w_out.shape[0]
        head_dim = w_out.shape[1]
        tokens = resid_x.shape[0]
        x_hat = (resid_x.astype(jnp.float32) - ln_mean[:, None]) * ln_rstd[:, None]
        gain_f32 = ln_gain.astype(jnp.float32)
        normed = (x_hat * gain_f32).astype(jnp.bfloat16)
        qkv_proj = jnp.dot(normed, w_qkv, preferred_element_type=jnp.float32).reshape(tokens, heads_local, 3, head_dim)
        rope_cos, rope_sin = rope_tables(tokens, head_dim // 4)
        q_rot = rotate(qkv_proj[..., 0, :], rope_cos, rope_sin).astype(jnp.bfloat16)
        k_rot = rotate(qkv_proj[..., 1, :], rope_cos, rope_sin).astype(jnp.bfloat16)
        values = qkv_proj[..., 2, :].astype(jnp.bfloat16)
        d_attn = jnp.einsum("te,hde->thd", grad_y, w_out, preferred_element_type=jnp.float32).astype(jnp.bfloat16)
        attn_out, d_q_rot, d_k_rot, d_values = attention_pair(q_rot, k_rot, values, d_attn)
        d_qkv = jnp.stack([rotate(d_q_rot, rope_cos, -rope_sin), rotate(d_k_rot, rope_cos, -rope_sin), d_values], axis=-2)
        d_qkv = d_qkv.astype(jnp.bfloat16).reshape(tokens, w_qkv.shape[1])
        grad_w_qkv = lax.dot_general(normed, d_qkv, CONTRACT_ROWS, preferred_element_type=jnp.float32).astype(jnp.bfloat16)
        grad_w_out = jnp.einsum("thd,te->hde", attn_out, grad_y, preferred_element_type=jnp.float32).astype(jnp.bfloat16)
        pre_act = jnp.dot(normed, w_up, preferred_element_type=jnp.float32)
        act_out, gelu_vjp = jax.vjp(exact_gelu, pre_act)
        act_bf = act_out.astype(jnp.bfloat16)
        grad_w_down = lax.dot_general(act_bf, grad_y, CONTRACT_ROWS, preferred_element_type=jnp.float32).astype(jnp.bfloat16)
        d_act = lax.dot_general(grad_y, w_down, CONTRACT_COLS, preferred_element_type=jnp.float32)
        d_pre = gelu_vjp(d_act)[0].astype(jnp.bfloat16)
        grad_w_up = lax.dot_general(normed, d_pre, CONTRACT_ROWS, preferred_element_type=jnp.float32).astype(jnp.bfloat16)
        part_sum = lax.dot_general(d_pre, w_up, CONTRACT_COLS, preferred_element_type=jnp.float32) + lax.dot_general(d_qkv, w_qkv, CONTRACT_COLS, preferred_element_type=jnp.float32)
        d_normed = lax.psum(part_sum.astype(jnp.bfloat16), "model").astype(jnp.float32)
        grad_x = ln_backward(d_normed, x_hat, gain_f32, ln_rstd, grad_y)
        return grad_x, grad_w_qkv, grad_w_out, grad_w_up, grad_w_down

    in_specs = (P("data", None), P("data"), P("data"), P(None), P("data", None), P(None, "model"), P("model", None, None), P(None, "model"), P("model", None))
    out_specs = (P("data", None), P("data", "model"), P(("data", "model"), None, None), P("data", "model"), P(("data", "model"), None))
    return jax.shard_map(device_step, mesh=mesh, in_specs=in_specs, out_specs=out_specs, check_vma=False)
```

profile of v0, /device:TPU:0, one launch (start us, length us, event | category | flops | bytes accessed | tf_op | source)
XLA Modules:
  0.0 817.7 jit_solution(17444335939561253373)
XLA Ops:
  7.2 0.0 copy-start
  7.2 0.0 all-reduce.2.cloned.1.call-start
  7.2 0.0 copy-start.12
  7.3 0.8 convert_element_type.91
  8.1 0.6 copy-done.6
  8.7 15.8 %multiply_convert_fusion.1 = bf16[4096,2048]{1,0:T(8,128)(2,1)} fusion(bf16[4096,2048]{1,0:T(8,128)(2,1)} %param.9, f32[2048]{0:T(1024)S(1)} %convert_element_type.91, f32[4096]{0:T(1024)} %param.10, f32[4096]{0:T(1024)} %param.11), kind=kLoop, calls=%fused_computation.13 | loop fusion | flops 41943040 | bytes 33595392 | tf_op jit(solution)/shard_map/convert_element_type | solution.py:61
  24.5 0.0 copy-done
  24.5 19.5 %fusion.53 = f32[4096,768]{0,1:T(8,128)} fusion(bf16[4096,2048]{1,0:T(8,128)(2,1)} %multiply_convert_fusion.1, bf16[2048,768]{1,0:T(8,128)(2,1)S(1)} %copy-done), kind=kOutput, calls=%fused_computation.92 | convolution fusion | flops 12884901888 | bytes 32505856 | tf_op jit(solution)/shard_map/dot_general | solution.py:62
  44.1 4.0 slice_bitcast_fusion.1
  48.1 2.1 fusion.31
  50.2 0.0 copy-done.12
  50.2 3.2 fusion.41
  53.4 28.2 %fusion.2 = (f32[4096]{0:T(1024)S(1)}, f32[4096,4096]{0,1:T(8,128)}) fusion(bf16[4096,192]{0,1:T(8,128)(2,1)} %get-tuple-element.27, bf16[4096,32]{0,1:T(8,128)(2,1)} %get-tuple-element.16, bf16[4096,32]{0,1:T(8,128)(2,1)} %get-tuple-element.15, bf16[4096,192]{0,1:T(8,128)(2,1)} %get-tuple-element.28, bf16[4096,32]{0,1:T(8,128)(2,1)S(1)} %get-tuple-element.21, ...), kind=kOutput, calls=%fused_computation.7 | convolution fusion | flops 8669622272 | bytes 71319552 | tf_op jit(solution)/shard_map/...qhd,...khd->...hqk/dot_general | solution.py:32
  81.6 21.8 %fusion.1 = f32[4096]{0:T(1024)S(1)} fusion(f32[4096,4096]{0,1:T(8,128)} %get-tuple-element.24, f32[4096]{0:T(1024)S(1)} %get-tuple-element.23), kind=kLoop, calls=%fused_computation.6 | loop fusion | flops 83881984 | bytes 67141632 | tf_op jit(solution)/shard_map/reduce_sum | solution.py:34
  103.4 11.9 %convolution_convert_fusion = bf16[4096,256]{1,0:T(8,128)(2,1)} fusion(bf16[4096,2048]{1,0:T(8,128)(2,1)} %param.13, bf16[1,256,2048]{2,1,0:T(8,128)(2,1)} %param.15), kind=kOutput, calls=%fused_computation.43 | convolution fusion | flops 4296015872 | bytes 19922944 | tf_op jit(solution)/shard_map/te,hde->thd/dot_general | solution.py:67
  115.3 50.7 %multiply_reduce_fusion = (f32[4096]{0:T(1024)S(1)}, f32[4096,4096]{0,1:T(8,128)}) fusion(f32[4096]{0:T(1024)S(1)} %fusion.1, f32[4096]{0:T(1024)S(1)} %get-tuple-element.23, f32[4096,4096]{0,1:T(8,128)} %get-tuple-element.24, bf16[4096,256]{1,0:T(8,128)(2,1)} %convolution_convert_fusion, f32[4096,1,3,256]{0,3,2,1:T(8,128)} %bitcast.81), kind=kOutput, calls=%fused_computation.1 | convolution fusion | flops 8707371008 | bytes 138461184 | tf_op jit(solution)/shard_map/...qhd,...khd->...hqk/dot_general | solution.py:37
  166.0 53.5 %multiply_convert_fusion = bf16[4096,4096]{0,1:T(8,128)(2,1)} fusion(f32[4096,4096]{0,1:T(8,128)} %get-tuple-element.26, f32[4096]{0:T(1024)S(1)} %get-tuple-element.25, f32[4096]{0:T(1024)S(1)} %fusion.1, f32[4096]{0:T(1024)S(1)} %get-tuple-element.23, f32[4096,4096]{0,1:T(8,128)} %get-tuple-element.24), kind=kLoop, calls=%fused_computation | loop fusion | flops 150994944 | bytes 167821312 | tf_op jit(solution)/shard_map/convert_element_type | solution.py:40
  219.4 17.0 %convolution_bitcast_fusion.1 = f32[4096,1,256]{0,2,1:T(8,128)} fusion(bf16[4096,4096]{0,1:T(8,128)(2,1)} %multiply_convert_fusion, bf16[4096,192]{0,1:T(8,128)(2,1)} %get-tuple-element.27, bf16[4096,32]{0,1:T(8,128)(2,1)} %get-tuple-element.16, bf16[4096,32]{0,1:T(8,128)(2,1)} %get-tuple-element.15), kind=kOutput, calls=%fused_computation.40 | convolution fusion | flops 8596226048 | bytes 39845888 | tf_op jit(solution)/shard_map/...hqk,...khd->...qhd/dot_general | solution.py:41
  236.4 17.5 %convolution_bitcast_fusion = f32[4096,1,256]{0,2,1:T(8,128)} fusion(bf16[4096,4096]{0,1:T(8,128)(2,1)} %multiply_convert_fusion, bf16[4096,192]{0,1:T(8,128)(2,1)} %get-tuple-element.28, bf16[4096,32]{0,1:T(8,128)(2,1)S(1)} %copy-done.3, bf16[4096,32]{0,1:T(8,128)(2,1)} %get-tuple-element.22), kind=kOutput, calls=%fused_computation.39 | convolution fusion | flops 8596226048 | bytes 39845888 | tf_op jit(solution)/shard_map/...hqk,...qhd->...khd/dot_general | solution.py:42
  253.9 3.3 slice.128
  257.2 4.2 subtract_convert_fusion.1
  261.4 3.2 slice.127
  264.7 30.9 %fusion.22 = bf16[4096,1,1,256]{0,3,2,1:T(8,128)(2,1)} fusion(bf16[4096,256]{1,0:T(8,128)(2,1)} %convolution_convert_fusion, f32[4096,4096]{0,1:T(8,128)} %get-tuple-element.24, f32[4096]{0:T(1024)S(1)} %fusion.1, f32[4096]{0:T(1024)S(1)} %get-tuple-element.23), kind=kOutput, calls=%fused_computation.44 | convolution fusion | flops 8691646464 | bytes 71335936 | tf_op jit(solution)/shard_map/...hqk,...qhd->...khd/dot_general | solution.py:38
  295.6 1.6 maximum_bitcast_fusion
  297.2 1.6 maximum_bitcast_fusion.1
  298.8 4.5 pad_maximum_fusion
  303.3 20.6 %fusion.54 = f32[4096,2048]{1,0:T(8,128)} fusion(bf16[4096,768]{0,1:T(8,128)(2,1)} %bitcast.78, bf16[2048,768]{1,0:T(8,128)(2,1)S(1)} %copy-done), kind=kOutput, calls=%fused_computation.93 | convolution fusion | flops 12884901888 | bytes 42991616 | tf_op jit(solution)/shard_map/dot_general | solution.py:80
  323.9 22.3 %fusion.52 = f32[4096,1024]{1,0:T(8,128)} fusion(bf16[4096,2048]{1,0:T(8,128)(2,1)} %multiply_convert_fusion.1, bf16[2048,1024]{1,0:T(8,128)(2,1)S(1)} %copy-done.15), kind=kOutput, calls=%fused_computation.91 | convolution fusion | flops 17179869184 | bytes 37748736 | tf_op jit(solution)/shard_map/dot_general | solution.py:73
  346.3 0.0 copy-done.14
  346.3 59.3 %add_convert_fusion.2 = (bf16[4096,1024]{1,0:T(8,128)(2,1)}, f32[4096,1024]{1,0:T(8,128)}) fusion(f32[4096,1024]{1,0:T(8,128)} %fusion.52, bf16[4096,2048]{1,0:T(8,128)(2,1)} %param.13, bf16[1024,2048]{1,0:T(8,128)(2,1)S(1)} %copy-done.14), kind=kOutput, calls=%fused_computation.22 | convolution fusion | flops 17481859072 | bytes 62914560 | tf_op jit(solution)/shard_map/dot_general | solution.py:77
  405.6 0.0 copy-done.16
  405.6 26.6 %add_convert_fusion.1 = bf16[4096,2048]{1,0:T(8,128)(2,1)} fusion(f32[4096,2048]{1,0:T(8,128)} %fusion.54, bf16[4096,1024]{1,0:T(8,128)(2,1)} %get-tuple-element.7, bf16[2048,1024]{1,0:T(8,128)(2,1)S(1)} %copy-done.16), kind=kOutput, calls=%fused_computation.12 | convolution fusion | flops 17196646400 | bytes 62914560 | tf_op jit(solution)/shard_map/dot_general | solution.py:80
  432.2 0.0 all-reduce.2.cloned.1.call-update
  432.2 0.7 copy-done.9
  432.9 0.0 copy-done.11
  432.9 29.7 %fusion.25 = bf16[4096,256]{0,1:T(8,128)(2,1)S(1)} fusion(f32[4096,1,3,256]{0,3,2,1:T(8,128)} %bitcast.82, f32[4096,4096]{0,1:T(8,128)} %get-tuple-element.24, f32[4096]{0:T(1024)S(1)} %copy-done.11, f32[4096]{0:T(1024)S(1)} %copy-done.9), kind=kOutput, calls=%fused_computation.45 | convolution fusion | flops 8691646464 | bytes 71335936 | tf_op jit(solution)/shard_map/...hqk,...khd->...qhd/dot_general | solution.py:36
  462.6 19.9 %convolution_convert_fusion.2 = bf16[2048,768]{1,0:T(8,128)(2,1)} fusion(bf16[4096,2048]{1,0:T(8,128)(2,1)} %multiply_convert_fusion.1, bf16[4096,768]{0,1:T(8,128)(2,1)} %bitcast.79), kind=kOutput, calls=%fused_computation.51 | convolution fusion | flops 12886474752 | bytes 26214400 | tf_op jit(solution)/shard_map/dot_general | solution.py:71
  482.5 9.4 %fusion.29 = bf16[1,256,2048]{2,1,0:T(8,128)(2,1)} fusion(bf16[4096,256]{0,1:T(8,128)(2,1)S(1)} %fusion.25, bf16[4096,2048]{1,0:T(8,128)(2,1)} %param.13), kind=kOutput, calls=%fused_computation.57 | convolution fusion | flops 4295491584 | bytes 19922944 | tf_op jit(solution)/shard_map/thd,te->hde/dot_general | solution.py:72
  491.8 27.7 %fusion.28 = bf16[1024,2048]{1,0:T(8,128)(2,1)} fusion(bf16[4096,2048]{1,0:T(8,128)(2,1)} %param.13, f32[4096,1024]{1,0:T(8,128)} %get-tuple-element.8, f32[4096,1024]{1,0:T(8,128)} %fusion.52), kind=kOutput, calls=%fused_computation.50 | convolution fusion | flops 17194549248 | bytes 54525952 | tf_op jit(solution)/shard_map/dot_general | solution.py:76
  519.6 0.0 copy-start.4
  519.6 0.0 copy-start.5
  519.6 21.2 %convolution_convert_fusion.1 = bf16[2048,1024]{1,0:T(8,128)(2,1)} fusion(bf16[4096,2048]{1,0:T(8,128)(2,1)} %multiply_convert_fusion.1, bf16[4096,1024]{1,0:T(8,128)(2,1)S(1)} %bitcast.84), kind=kOutput, calls=%fused_computation.49 | convolution fusion | flops 17181966336 | bytes 29360128 | tf_op jit(solution)/shard_map/dot_general | solution.py:79
  540.8 226.9 %all-reduce.2.cloned.1.call-done = bf16[4096,2048]{1,0:T(8,128)(2,1)} async-done(((bf16[4096,2048]{1,0:T(8,128)(2,1)}), bf16[4096,2048]{1,0:T(8,128)(2,1)}) %all-reduce.2.cloned.1.call-update) | async-done | bytes 16777232 | tf_op jit(solution)/shard_map/psum | solution.py:81
  767.7 0.0 copy-done.5
  767.7 16.2 %fusion.3 = (f32[4096]{0:T(1024)S(1)}, f32[4096]{0:T(1024)S(1)}) fusion(bf16[4096,2048]{1,0:T(8,128)(2,1)} %all-reduce.2.cloned.1.call-done, f32[2048]{0:T(1024)S(1)} %copy-done.7, f32[4096]{0:T(1024)S(1)} %copy-done.5, f32[4096]{0:T(1024)S(1)} %copy-done.4, bf16[4096,2048]{1,0:T(8,128)(2,1)} %param.9), kind=kLoop, calls=%fused_computation.11 | loop fusion | flops 67100672 | bytes 33628160 | tf_op jit(solution)/shard_map/reduce_sum | solution.py:48
  783.9 0.0 copy-start.1
  783.9 26.5 %add_convert_fusion = bf16[4096,2048]{1,0:T(8,128)(2,1)} fusion(bf16[4096,2048]{1,0:T(8,128)(2,1)} %all-reduce.2.cloned.1.call-done, bf16[4096,2048]{1,0:T(8,128)(2,1)} %param.9, bf16[4096,2048]{1,0:T(8,128)(2,1)} %param.13, f32[4096]{0:T(1024)S(1)} %broadcast_multiply_fusion, f32[4096]{0:T(1024)S(1)} %broadcast_multiply_fusion.1, f32[2048]{0:T(1024)S(1)} %copy-done.7, ...), kind=kLoop, calls=%fused_computation.8 | loop fusion | flops 100663296 | bytes 67182592 | tf_op jit(solution)/shard_map/convert_element_type | solution.py:51
  810.4 0.0 copy-done.1
  (28 shorter events, 0.1 us)
Async XLA Ops:
  7.2 17.4 %copy-start = (bf16[2048,768]{1,0:T(8,128)(2,1)S(1)}, bf16[2048,768]{1,0:T(8,128)(2,1)}, u32[]{:S(2)}) copy-start(bf16[2048,768]{1,0:T(8,128)(2,1)} %param.14) | copy-start | bytes 9437188
  7.2 760.5 %all-reduce.2.cloned.1.call-start = ((), (), s32[]{:S(2)}) async-start(), calls=%async_computation | async-start | bytes 33554432 | tf_op jit(solution)/shard_map/psum | solution.py:81
  7.2 42.9 %copy-start.12 = (f32[32]{0:T(128)}, f32[32]{0:T(128)S(1)}, u32[]{:S(2)}) copy-start(f32[32]{0:T(128)S(1)} %multiply_power_fusion) | copy-start | bytes 388
  8.1 0.6 copy-start.6
  53.4 28.2 %copy-start.2 = (bf16[4096,32]{0,1:T(8,128)(2,1)}, bf16[4096,32]{0,1:T(8,128)(2,1)S(1)}, u32[]{:S(2)}) copy-start(bf16[4096,32]{0,1:T(8,128)(2,1)S(1)} %get-tuple-element.21) | copy-start | bytes 786436
  81.6 183.1 %copy-start.8 = (f32[4096]{0:T(1024)}, f32[4096]{0:T(1024)S(1)}, u32[]{:S(2)}) copy-start(f32[4096]{0:T(1024)S(1)} %get-tuple-element.23) | copy-start | bytes 49156
  103.4 161.3 %copy-start.10 = (f32[4096]{0:T(1024)}, f32[4096]{0:T(1024)S(1)}, u32[]{:S(2)}) copy-start(f32[4096]{0:T(1024)S(1)} %fusion.1) | copy-start | bytes 49156
  219.4 17.0 %copy-start.3 = (bf16[4096,32]{0,1:T(8,128)(2,1)S(1)}, bf16[4096,32]{0,1:T(8,128)(2,1)}, u32[]{:S(2)}) copy-start(bf16[4096,32]{0,1:T(8,128)(2,1)} %copy-done.2) | copy-start | bytes 786436
  236.4 20.8 %copy-start.13 = (f32[32]{0:T(128)S(1)}, f32[32]{0:T(128)}, u32[]{:S(2)}) copy-start(f32[32]{0:T(128)} %copy-done.12) | copy-start | bytes 388
  303.3 20.6 %copy-start.15 = (bf16[2048,1024]{1,0:T(8,128)(2,1)S(1)}, bf16[2048,1024]{1,0:T(8,128)(2,1)}, u32[]{:S(2)}) copy-start(bf16[2048,1024]{1,0:T(8,128)(2,1)} %param.16) | copy-start | bytes 12582916
  323.9 22.4 %copy-start.14 = (bf16[1024,2048]{1,0:T(8,128)(2,1)S(1)}, bf16[1024,2048]{1,0:T(8,128)(2,1)}, u32[]{:S(2)}) copy-start(bf16[1024,2048]{1,0:T(8,128)(2,1)} %param.17) | copy-start | bytes 12582916
  346.3 59.3 %copy-start.16 = (bf16[2048,1024]{1,0:T(8,128)(2,1)S(1)}, bf16[2048,1024]{1,0:T(8,128)(2,1)}, u32[]{:S(2)}) copy-start(bf16[2048,1024]{1,0:T(8,128)(2,1)} %param.16) | copy-start | bytes 12582916
  432.2 0.7 copy-start.9
  432.2 0.7 copy-start.11
  482.5 37.1 %slice-start = ((s8[8388608]{0:T(1024)(128)(4,1)}), s8[4194304]{0:T(1024)(128)(4,1)S(1)}, s32[]{:S(2)}) async-start(s8[8388608]{0:T(1024)(128)(4,1)} %bitcast.83), calls=%async_computation.1 | async-start | bytes 8388608
  491.8 27.7 %slice-start.1 = ((s8[8388608]{0:T(1024)(128)(4,1)}), s8[4194304]{0:T(1024)(128)(4,1)S(1)}, s32[]{:S(2)}) async-start(s8[8388608]{0:T(1024)(128)(4,1)} %bitcast.83), calls=%async_computation.2 | async-start | bytes 8388608
  519.6 248.1 %copy-start.4 = (f32[4096]{0:T(1024)S(1)}, f32[4096]{0:T(1024)}, u32[]{:S(2)}) copy-start(f32[4096]{0:T(1024)} %param.10) | copy-start | bytes 49156
  519.6 248.1 %copy-start.5 = (f32[4096]{0:T(1024)S(1)}, f32[4096]{0:T(1024)}, u32[]{:S(2)}) copy-start(f32[4096]{0:T(1024)} %param.11) | copy-start | bytes 49156
  519.6 248.1 %copy-start.7 = (f32[2048]{0:T(1024)S(1)}, f32[2048]{0:T(1024)}, u32[]{:S(2)}) copy-start(f32[2048]{0:T(1024)} %copy-done.6) | copy-start | bytes 24580
  783.9 26.5 %copy-start.1 = (bf16[2048,768]{1,0:T(8,128)(2,1)S(1)}, bf16[2048,768]{1,0:T(8,128)(2,1)}, u32[]{:S(2)}) copy-start(bf16[2048,768]{1,0:T(8,128)(2,1)} %param.14) | copy-start | bytes 9437188
Sparse Core Ops, SparseCore 0:
  432.3 335.3 all-reduce.1
where the time goes:
time: 825 us; the launch traced here: 818 us
  matrix products  412 us (50%)
  waiting for transfers between devices  227 us (28%)
  other arithmetic  150 us (18%)
  between operations  14.6 us (2%)
  local copies, waits for them, and re-layouts  14 us (2%)
    psum x1, waiting for transfers between devices, device_step(): lax.psum(part_sum.astype(jnp.bfloat16), 'model').astype(jnp.float32)  227 us
    dot_general x1, matrix products, device_step(): lax.dot_general(grad_y, w_down, CONTRACT_COLS, preferred_element_type=jnp...  59.3 us
    convert_element_type x1, other arithmetic, attention_pair(): (attn_probs * (d_probs - row_delta) * att_scale).astype(jnp.bfloat16)  53.5 us
    dot_general x1, matrix products, attention_pair(): jnp.einsum('...qhd,...khd->...hqk', d_attn, values, preferred_element_typ...  50.7 us
    dot_general x1, matrix products, attention_pair(): jnp.einsum('...hqk,...qhd->...khd', probs_bf, d_attn, preferred_element_t...  30.9 us
    dot_general x1, matrix products, attention_pair(): jnp.einsum('...hqk,...khd->...qhd', probs_bf, values, preferred_element_t...  29.7 us
    dot_general x1, matrix products, attention_pair(): jnp.einsum('...qhd,...khd->...hqk', q_rot, k_rot, preferred_element_type=...  28.2 us
    dot_general x1, matrix products, device_step(): lax.dot_general(act_bf, grad_y, CONTRACT_ROWS, preferred_element_type=jnp...  27.7 us
  transfers between devices with their start and end apart: 1, of which 1 were waited for; matrix products, arithmetic and copies ran while one was open for 13% of the time, Pallas kernels for 0%

commit v1 on v0

v1 whole, which is shorter than its diff:
```python
import functools

import jax
import jax.numpy as jnp
import numpy as np
from jax import lax
from jax.experimental import pallas as pl
from jax.experimental.pallas import tpu as pltpu
from jax.sharding import PartitionSpec as P

MESH = pl.DeviceIdType.MESH
F32, BF16 = jnp.float32, jnp.bfloat16
ROWS = 256
NEG = -1e30


def mm(a, b):
    return jnp.dot(a, b, preferred_element_type=F32)


def mm_nt(a, b):
    return lax.dot_general(a, b, (((1,), (1,)), ((), ())), preferred_element_type=F32)


def mm_tn(a, b):
    return lax.dot_general(a, b, (((0,), (0,)), ((), ())), preferred_element_type=F32)


def clip(v, hi):
    return jnp.minimum(jnp.maximum(v, 0), hi)


def layer_kernel(dims, x_hbm, dy_hbm, g_ref, cb_ref, sb_ref, co_ref, so_ref, wqkv_hbm, wo_hbm, w1_hbm, w2_hbm,
                 dx_hbm, dwqkv_hbm, dwo_hbm, dw1_hbm, dw2_hbm, n_hbm, g_hbm, da_hbm, dqkv_hbm, o_hbm, zin_hbm, xin_hbm,
                 qbuf, pst, sib_in, zst, xst, lx, ly,
                 sib_s, sib_r, qs_s, z_r, x_r, dxl_s, dxs_s, dxo_s, dxo_r, dxs_r, st_sem, in_sem, w_sem, out_sem, t2_sem):
    T, D, F, H, C = dims
    R = ROWS
    HALF = R // 2
    NB = T // R
    QPC = C // R
    me = lax.axis_index("model")
    core = lax.rem(me, 2)
    z = me // 2
    nbz = z + 1 - 2 * lax.rem(z, 2)
    sibling = z * 2 + 1 - core
    near = nbz * 2 + core
    partner = (3 - z) * 2 + core
    is_mid = (z == 1) | (z == 2)
    is_out = (z == 0) | (z == 3)

    barrier = pltpu.get_barrier_semaphore()
    pl.semaphore_signal(barrier, inc=1, device_id={"model": sibling}, device_id_type=MESH)
    pl.semaphore_signal(barrier, inc=1, device_id={"model": near}, device_id_type=MESH)

    @pl.when(is_mid)
    def _():
        pl.semaphore_signal(barrier, inc=1, device_id={"model": partner}, device_id_type=MESH)
        pl.semaphore_wait(barrier, 3)

    @pl.when(is_out)
    def _():
        pl.semaphore_wait(barrier, 2)

    def rows_of(t, c):
        return pl.ds(pl.multiple_of((NB - 1 - t) * R + c * HALF, HALF), HALF)

    def sib_copy(t):
        s = lax.rem(t, 2)
        return pltpu.make_async_remote_copy(src_ref=pst.at[pl.ds(pl.multiple_of((1 - core) * HALF, HALF), HALF)], dst_ref=sib_in.at[s],
                                            send_sem=sib_s.at[s], recv_sem=sib_r.at[s], device_id={"model": sibling}, device_id_type=MESH)

    def q_copy(t):
        return pltpu.make_async_remote_copy(src_ref=qbuf.at[t], dst_ref=zin_hbm.at[t], send_sem=qs_s.at[t], recv_sem=z_r.at[t],
                                            device_id={"model": near}, device_id_type=MESH)

    def x_copy(t):
        return pltpu.make_async_remote_copy(src_ref=qbuf.at[t], dst_ref=xin_hbm.at[t], send_sem=qs_s.at[t], recv_sem=x_r.at[t],
                                            device_id={"model": partner}, device_id_type=MESH)

    def dx_local(t):
        return pltpu.make_async_copy(qbuf.at[t], dx_hbm.at[rows_of(t, core)], dxl_s.at[t])

    def dx_sib(t):
        return pltpu.make_async_remote_copy(src_ref=qbuf.at[t], dst_ref=dx_hbm.at[rows_of(t, core)], send_sem=dxs_s.at[t], recv_sem=dxs_r.at[t],
                                            device_id={"model": sibling}, device_id_type=MESH)

    def dx_out(t):
        return pltpu.make_async_remote_copy(src_ref=qbuf.at[t], dst_ref=dx_hbm.at[rows_of(t, core)], send_sem=dxo_s.at[t], recv_sem=dxo_r.at[t],
                                            device_id={"model": near}, device_id_type=MESH)

    def dx_fwd(t):
        return pltpu.make_async_remote_copy(src_ref=dx_hbm.at[rows_of(t, core)], dst_ref=dx_hbm.at[rows_of(t, core)], send_sem=dxs_s.at[t],
                                            recv_sem=dxs_r.at[t], device_id={"model": sibling}, device_id_type=MESH)

    def z_load(t):
        return pltpu.make_async_copy(zin_hbm.at[t], zst, st_sem.at[0])

    def x_load(t):
        return pltpu.make_async_copy(xin_hbm.at[t], xst, st_sem.at[1])

    def lx_load(t):
        return pltpu.make_async_copy(x_hbm.at[rows_of(t, core)], lx, st_sem.at[2])

    def ly_load(t):
        return pltpu.make_async_copy(dy_hbm.at[rows_of(t, core)], ly, st_sem.at[3])

    def pair_sum(t):
        cp = sib_copy(t)
        cp.wait_send()
        cp.wait_recv()
        own = pst[pl.ds(pl.multiple_of(core * HALF, HALF), HALF), :].astype(F32)
        qbuf[t] = (own + sib_in[lax.rem(t, 2)].astype(F32)).astype(BF16)

        @pl.when(is_out)
        def _():
            q_copy(t).start()

    def e3_fetch(t):
        q_copy(t).wait_recv()
        z_load(t).start()

    def e3_process(t):
        z_load(t).wait()
        qbuf[t] = (qbuf[t].astype(F32) + zst[...].astype(F32)).astype(BF16)
        x_copy(t).start()

    def e4_fetch(t):
        x_copy(t).wait_recv()
        x_load(t).start()
        lx_load(t).start()
        ly_load(t).start()

    def e4_process(t):
        x_load(t).wait()
        lx_load(t).wait()
        ly_load(t).wait()
        x_copy(t).wait_send()
        xv = lx[...].astype(F32)
        mean = jnp.sum(xv, axis=1, keepdims=True) * (1.0 / D)
        xc = xv - mean
        rstd = lax.rsqrt(jnp.sum(xc * xc, axis=1, keepdims=True) * (1.0 / D) + 1e-5)
        xh = xc * rstd
        d = (qbuf[t].astype(F32) + xst[...].astype(F32)) * g_ref[...]
        md = jnp.sum(d, axis=1, keepdims=True) * (1.0 / D)
        mdx = jnp.sum(d * xh, axis=1, keepdims=True) * (1.0 / D)
        qbuf[t] = (ly[...].astype(F32) + rstd * (d - md - xh * mdx)).astype(BF16)
        dx_out(t).start()
        dx_sib(t).start()
        dx_local(t).start()

    def e5(t):
        dx_out(t).wait_recv()
        dx_fwd(t).start()

    def service_fetch(lo3, hi3, lo4, hi4, lo5, hi5):
        @pl.when(is_mid & (hi3 > lo3))
        def _():
            e3_fetch(lo3)

        @pl.when(is_mid & (hi4 > lo4))
        def _():
            e4_fetch(lo4)

        @pl.when(is_out & (hi5 > lo5))
        def _():
            e5(lo5)

    def service_process(lo3, hi3, lo4, hi4, lo5, hi5):
        @pl.when(is_mid & (hi3 > lo3))
        def _():
            e3_process(lo3)

        @pl.when(is_mid & (hi4 > lo4))
        def _():
            e4_process(lo4)

    def n_phase1(u, lag):
        return clip((5 * (u - lag) + 5) // 6, NB)

    LAG3, LAG4, LAG5 = 2, 4, 6

    def ticks1(u):
        return (n_phase1(u - 1, LAG3), n_phase1(u, LAG3), n_phase1(u - 1, LAG4), n_phase1(u, LAG4), n_phase1(u - 1, LAG5), n_phase1(u, LAG5))

    def n_phase2(w, lag):
        return jnp.minimum(n_phase1(NB - 1, lag) + (2 * (w + 1)) // 5, NB)

    def ticks2(w):
        return (n_phase2(w - 1, LAG3), n_phase2(w, LAG3), n_phase2(w - 1, LAG4), n_phase2(w, LAG4), n_phase2(w - 1, LAG5), n_phase2(w, LAG5))

    def rope_of(i):
        cb, sb = cb_ref[pl.ds(i, 1), :], sb_ref[pl.ds(i, 1), :]
        co, so = co_ref[...], so_ref[...]
        return cb * co - sb * so, sb * co + cb * so

    def rope(x, cosf, sinf):
        x0 = x[:, :128]
        lane = lax.broadcasted_iota(jnp.int32, x0.shape, 1)
        other = jnp.where(lane < H // 8, pltpu.roll(x0, 128 - H // 8, 1), pltpu.roll(x0, H // 8, 1))
        return jnp.concatenate([x0 * cosf + other * sinf, x[:, 128:]], axis=1)

    def attention_phase(kv, kT, vv, vT, dk, dv, es, dps, w1, w2, wqkv, wo, nbuf, ybuf, gst, dast, dqkvst, ost, qs, qT, do, doT, oT, dqT, msc):
        w_loads = [pltpu.make_async_copy(s, d_, w_sem.at[k]) for k, (s, d_) in enumerate(((wqkv_hbm, wqkv), (wo_hbm, wo), (w1_hbm, w1), (w2_hbm, w2)))]

        def blk(i):
            return pl.ds(pl.multiple_of(i * R, R), R)

        def x_in(b):
            return pltpu.make_async_copy(x_hbm.at[blk(b)], ybuf.at[lax.rem(b, 2)], in_sem.at[0, lax.rem(b, 2)])

        def n_out(b):
            return pltpu.make_async_copy(nbuf.at[lax.rem(b, 2)], n_hbm.at[blk(b)], out_sem.at[0, lax.rem(b, 2)])

        w_loads[0].start()
        x_in(0).start()
        for w in w_loads[1:]:
            w.start()
        dk[...] = jnp.zeros_like(dk)
        dv[...] = jnp.zeros_like(dv)
        w_loads[0].wait()

        @pl.loop(0, NB)
        def _(b):
            slot = lax.rem(b, 2)
            x_in(b).wait()

            @pl.when(b + 1 < NB)
            def _():
                x_in(b + 1).start()

            @pl.when(b >= 2)
            def _():
                n_out(b - 2).wait()

            xv = ybuf[slot].astype(F32)
            mean = jnp.sum(xv, axis=1, keepdims=True) * (1.0 / D)
            xc = xv - mean
            rstd = lax.rsqrt(jnp.sum(xc * xc, axis=1, keepdims=True) * (1.0 / D) + 1e-5)
            nbuf[slot] = ((xc * rstd) * g_ref[...]).astype(BF16)
            n_out(b).start()
            kvp = mm(nbuf[slot], wqkv[:, H:])
            cosf, sinf = rope_of(b)
            kf = rope(kvp[:, :H], cosf, sinf)
            vf = kvp[:, H:]
            kv[blk(b), :] = kf.astype(BF16)
            vv[blk(b), :] = vf.astype(BF16)
            kT[:, blk(b)] = kf.T.astype(BF16)
            vT[:, blk(b)] = vf.T.astype(BF16)

        n_out(NB - 2).wait()
        n_out(NB - 1).wait()

        def n_in(t):
            return pltpu.make_async_copy(n_hbm.at[blk(NB - 1 - t)], nbuf.at[lax.rem(t, 2)], in_sem.at[1, lax.rem(t, 2)])

        def y_in(t):
            return pltpu.make_async_copy(dy_hbm.at[blk(NB - 1 - t)], ybuf.at[lax.rem(t, 2)], in_sem.at[0, lax.rem(t, 2)])

        def outs(t):
            s, i = lax.rem(t, 2), NB - 1 - t
            return [pltpu.make_async_copy(gst.at[s], g_hbm.at[blk(i)], out_sem.at[0, s]),
                    pltpu.make_async_copy(dast.at[s], da_hbm.at[blk(i)], out_sem.at[1, s]),
                    pltpu.make_async_copy(dqkvst.at[s], dqkv_hbm.at[blk(i)], out_sem.at[2, s]),
                    pltpu.make_async_copy(ost.at[s], o_hbm.at[blk(i)], out_sem.at[3, s])]

        n_in(0).start()
        y_in(0).start()
        for w in w_loads[1:]:
            w.wait()

        @pl.loop(0, NB)
        def _(t):
            slot = lax.rem(t, 2)
            i = NB - 1 - t
            n_in(t).wait()
            y_in(t).wait()

            @pl.when(t + 1 < NB)
            def _():
                n_in(t + 1).start()
                y_in(t + 1).start()

            @pl.when(t >= 2)
            def _():
                for cp in outs(t - 2):
                    cp.wait()

            service_fetch(*ticks1(t))

            FT = min(512, F)
            for f in range(0, F, FT):
                a = mm(nbuf[slot], w1[:, f:f + FT])
                da = mm_nt(ybuf[slot], w2[f:f + FT, :])
                phi = 0.5 + 0.5 * lax.erf(a * 0.7071067811865476)
                gst[slot, :, f:f + FT] = (a * phi).astype(BF16)
                dast[slot, :, f:f + FT] = (da * (phi + a * (0.3989422804014327 * jnp.exp(-0.5 * (a * a))))).astype(BF16)
            for cp in outs(t)[:2]:
                cp.start()

            @pl.when(t > 0)
            def _():
                pair_sum(t - 1)

            service_process(*ticks1(t))

            cosf, sinf = rope_of(i)
            qf = rope(mm(nbuf[slot], wqkv[:, :H]), cosf, sinf).astype(BF16).astype(F32) * (H ** -0.5)
            qs[...] = qf.astype(BF16)
            qT[...] = qf.T.astype(BF16)
            dof = mm_nt(ybuf[slot], wo[...])
            do[...] = dof.astype(BF16)
            doT[...] = dof.T.astype(BF16)
            nfull = i // QPC

            def chunk(j):
                return pl.ds(pl.multiple_of(j * C, C), C)

            def pass_a(j, carry, masked):
                m, l, dl = carry
                st = mm(kv[chunk(j), :], qT[...])
                if masked:
                    key = j * C + lax.broadcasted_iota(jnp.int32, st.shape, 0)
                    query = i * R + lax.broadcasted_iota(jnp.int32, st.shape, 1)
                    st = jnp.where(key <= query, st, NEG)
                dp = mm(vv[chunk(j), :], doT[...])
                m_new = jnp.maximum(m, jnp.max(st, axis=0, keepdims=True))
                alpha = jnp.exp(m - m_new)
                e = jnp.exp(st - m_new)
                es[chunk(j), :] = e
                dps[chunk(j), :] = dp
                msc[pl.ds(j, 1), :] = m_new
                return m_new, l * alpha + jnp.sum(e, axis=0, keepdims=True), dl * alpha + jnp.sum(e * dp, axis=0, keepdims=True)

            init = (jnp.full((1, R), NEG, F32), jnp.zeros((1, R), F32), jnp.zeros((1, R), F32))
            carry = lax.fori_loop(0, nfull, functools.partial(pass_a, masked=False), init)
            m, l, dl = pass_a(nfull, carry, True)
            inv_l = 1.0 / l
            delta = dl * inv_l
            oT[...] = jnp.zeros_like(oT)
            dqT[...] = jnp.zeros_like(dqT)

            @pl.loop(0, nfull + 1)
            def _(j):
                p = es[chunk(j), :] * (jnp.exp(msc[pl.ds(j, 1), :] - m) * inv_l)
                pb = p.astype(BF16)
                ds = (p * (dps[chunk(j), :] - delta)).astype(BF16)
                oT[...] += mm(vT[:, chunk(j)], pb)
                dqT[...] += mm(kT[:, chunk(j)], ds)
                dv[chunk(j), :] += mm(pb, do[...])
                dk[chunk(j), :] += mm(ds, qs[...])

            ost[slot] = oT[...].T.astype(BF16)
            dqkvst[slot, :, :H] = rope(dqT[...].T * (H ** -0.5), cosf, -sinf).astype(BF16)
            dqkvst[slot, :, H:2 * H] = rope(dk[blk(i), :], cosf, -sinf).astype(BF16)
            dqkvst[slot, :, 2 * H:] = dv[blk(i), :].astype(BF16)
            for cp in outs(t)[2:]:
                cp.start()

            DT = min(512, D)
            for c in range(0, D, DT):
                pst[:, c:c + DT] = (mm_nt(dast[slot], w1[c:c + DT, :]) + mm_nt(dqkvst[slot], wqkv[c:c + DT, :])).astype(BF16)
            sib_copy(t).start()

        for t in (NB - 2, NB - 1):
            for cp in outs(t):
                cp.wait()

    pl.run_scoped(
        attention_phase,
        pltpu.VMEM((T, H), BF16), pltpu.VMEM((H, T), BF16), pltpu.VMEM((T, H), BF16), pltpu.VMEM((H, T), BF16),
        pltpu.VMEM((T, H), F32), pltpu.VMEM((T, H), F32), pltpu.VMEM((T, R), F32), pltpu.VMEM((T, R), F32),
        pltpu.VMEM((D, F), BF16), pltpu.VMEM((F, D), BF16), pltpu.VMEM((D, 3 * H), BF16), pltpu.VMEM((H, D), BF16),
        pltpu.VMEM((2, R, D), BF16), pltpu.VMEM((2, R, D), BF16), pltpu.VMEM((2, R, F), BF16), pltpu.VMEM((2, R, F), BF16),
        pltpu.VMEM((2, R, 3 * H), BF16), pltpu.VMEM((2, R, H), BF16),
        pltpu.VMEM((R, H), BF16), pltpu.VMEM((H, R), BF16), pltpu.VMEM((R, H), BF16), pltpu.VMEM((H, R), BF16),
        pltpu.VMEM((H, R), F32), pltpu.VMEM((H, R), F32), pltpu.VMEM((8, R), F32))

    NT1, NT2 = D // H, F // H

    def weight_phase(da, dqkv, dy, nt, w1st, wqst, w2st):
        loads = [pltpu.make_async_copy(s, d_, w_sem.at[k]) for k, (s, d_) in enumerate(((da_hbm, da), (dqkv_hbm, dqkv), (dy_hbm, dy)))]

        def cols(m):
            return pl.ds(pl.multiple_of(m * H, H), H)

        def nt_in(m):
            return pltpu.make_async_copy(n_hbm.at[:, cols(m)], nt.at[lax.rem(m, 2)], t2_sem.at[0, lax.rem(m, 2)])

        def g_in(m):
            return pltpu.make_async_copy(g_hbm.at[:, cols(m)], nt.at[lax.rem(m, 2)], t2_sem.at[0, lax.rem(m, 2)])

        def o_in():
            return pltpu.make_async_copy(o_hbm, nt.at[NT2 % 2], t2_sem.at[0, NT2 % 2])

        def out1(m):
            s = lax.rem(m, 2)
            return [pltpu.make_async_copy(w1st.at[s], dw1_hbm.at[cols(m)], t2_sem.at[1, s]),
                    pltpu.make_async_copy(wqst.at[s], dwqkv_hbm.at[cols(m)], t2_sem.at[2, s])]

        def out2(m):
            return pltpu.make_async_copy(w2st.at[lax.rem(m, 2)], dw2_hbm.at[cols(m)], t2_sem.at[1, lax.rem(m, 2)])

        def out3():
            return pltpu.make_async_copy(w2st.at[NT2 % 2], dwo_hbm, t2_sem.at[1, NT2 % 2])

        loads[0].start()
        nt_in(0).start()
        loads[1].start()
        loads[2].start()
        pair_sum(NB - 1)
        loads[0].wait()
        loads[1].wait()

        @pl.loop(0, NT1)
        def _(m):
            s = lax.rem(m, 2)
            nt_in(m).wait()

            @pl.when(m + 1 < NT1)
            def _():
                nt_in(m + 1).start()

            @pl.when(m + 1 == NT1)
            def _():
                g_in(0).start()

            @pl.when(m >= 2)
            def _():
                for cp in out1(m - 2):
                    cp.wait()

            service_fetch(*ticks2(m))
            w1st[s] = mm_tn(nt[s], da[...]).astype(BF16)
            wqst[s] = mm_tn(nt[s], dqkv[...]).astype(BF16)
            for cp in out1(m):
                cp.start()
            service_process(*ticks2(m))

        for m in (NT1 - 2, NT1 - 1):
            for cp in out1(m):
                cp.wait()
        loads[2].wait()

        @pl.loop(0, NT2)
        def _(m):
            s = lax.rem(m, 2)
            g_in(m).wait()

            @pl.when(m + 1 < NT2)
            def _():
                g_in(m + 1).start()

            @pl.when(m + 1 == NT2)
            def _():
                o_in().start()

            @pl.when(m >= 2)
            def _():
                out2(m - 2).wait()

            service_fetch(*ticks2(NT1 + m))
            w2st[s] = mm_tn(nt[s], dy[...]).astype(BF16)
            out2(m).start()
            service_process(*ticks2(NT1 + m))

        o_in().wait()
        out2(NT2 - 2).wait()
        service_fetch(*ticks2(NT1 + NT2))
        w2st[NT2 % 2] = mm_tn(nt[NT2 % 2], dy[...]).astype(BF16)
        out3().start()
        service_process(*ticks2(NT1 + NT2))
        out2(NT2 - 1).wait()
        out3().wait()

    pl.run_scoped(
        weight_phase,
        pltpu.VMEM((T, F), BF16), pltpu.VMEM((T, 3 * H), BF16), pltpu.VMEM((T, D), BF16), pltpu.VMEM((2, T, H), BF16),
        pltpu.VMEM((2, H, F), BF16), pltpu.VMEM((2, H, 3 * H), BF16), pltpu.VMEM((2, H, D), BF16))

    WL = NT1 + NT2
    l3, l4, l5 = n_phase2(WL, LAG3), n_phase2(WL, LAG4), n_phase2(WL, LAG5)

    @pl.when(is_mid)
    def _():
        @pl.loop(0, NB - l4)
        def _(k):
            @pl.when(l3 + k < NB)
            def _():
                e3_fetch(l3 + k)
                e3_process(l3 + k)

            e4_fetch(l4 + k)
            e4_process(l4 + k)

        @pl.loop(0, NB)
        def _(t):
            dx_local(t).wait()
            dx_sib(t).wait_send()
            dx_out(t).wait_send()
            dx_sib(t).wait_recv()

    @pl.when(is_out)
    def _():
        @pl.loop(l5, NB)
        def _(t):
            e5(t)

        @pl.loop(0, NB)
        def _(t):
            q_copy(t).wait_send()
            dx_fwd(t).wait_send()
            dx_fwd(t).wait_recv()


def rope_tables(blocks, head_dim):
    rot = head_dim // 4
    half = rot // 2
    inv_freq = np.power(np.float32(10000.0), (-2.0 * np.arange(half, dtype=np.float32) / rot).astype(np.float32)).astype(np.float64)
    freq = np.zeros((1, 128))
    freq[0, :half], freq[0, half:rot] = -inv_freq, inv_freq
    at = np.arange(blocks)[:, None] * ROWS * freq
    off = np.arange(ROWS)[:, None] * freq
    return [np.asarray(t, np.float32) for t in (np.cos(at), np.sin(at), np.cos(off), np.sin(off))]


def solution(mesh):
    def device_step(resid_x, ln_mean, ln_rstd, ln_gain, grad_y, w_qkv, w_out, w_up, w_down):
        T, D = resid_x.shape
        F = w_up.shape[1]
        H = w_out.shape[1]
        NB = T // ROWS
        HALF = ROWS // 2
        C = min(1024, T)
        tabs = [jnp.asarray(t) for t in rope_tables(NB, H)]
        any_spec = pl.BlockSpec(memory_space=pl.ANY)
        vmem = pl.BlockSpec(memory_space=pltpu.VMEM)
        sds = lambda *s: jax.ShapeDtypeStruct(s, BF16)
        outs = pl.pallas_call(
            functools.partial(layer_kernel, (T, D, F, H, C)),
            name="layer_backward",
            out_shape=[sds(T, D), sds(D, 3 * H), sds(H, D), sds(D, F), sds(F, D),
                       sds(T, D), sds(T, F), sds(T, F), sds(T, 3 * H), sds(T, H), sds(NB, HALF, D), sds(NB, HALF, D)],
            in_specs=[any_spec, any_spec, vmem, vmem, vmem, vmem, vmem, any_spec, any_spec, any_spec, any_spec],
            out_specs=[any_spec] * 12,
            scratch_shapes=[
                pltpu.VMEM((NB, HALF, D), BF16), pltpu.VMEM((ROWS, D), BF16), pltpu.VMEM((2, HALF, D), BF16),
                pltpu.VMEM((HALF, D), BF16), pltpu.VMEM((HALF, D), BF16), pltpu.VMEM((HALF, D), BF16), pltpu.VMEM((HALF, D), BF16),
                pltpu.SemaphoreType.DMA((2,)), pltpu.SemaphoreType.DMA((2,))]
            + [pltpu.SemaphoreType.DMA((NB,))] * 8
            + [pltpu.SemaphoreType.DMA((4,)), pltpu.SemaphoreType.DMA((2, 2)), pltpu.SemaphoreType.DMA((4,)), pltpu.SemaphoreType.DMA((4, 2)),
               pltpu.SemaphoreType.DMA((3, 2))],
            compiler_params=pltpu.CompilerParams(collective_id=0, has_side_effects=True, vmem_limit_bytes=67043328),
        )(resid_x, grad_y, ln_gain.astype(F32).reshape(1, D), *tabs, w_qkv, w_out.reshape(H, D), w_up, w_down)
        grad_x, grad_w_qkv, grad_w_out, grad_w_up, grad_w_down = outs[:5]
        return grad_x, grad_w_qkv, grad_w_out.reshape(1, H, D), grad_w_up, grad_w_down

    in_specs = (P("data", None), P("data"), P("data"), P(None), P("data", None), P(None, "model"), P("model", None, None), P(None, "model"), P("model", None))
    out_specs = (P("data", None), P("data", "model"), P(("data", "model"), None, None), P("data", "model"), P(("data", "model"), None))
    return jax.shard_map(device_step, mesh=mesh, in_specs=in_specs, out_specs=out_specs, check_vma=False)
```

time: 825 us -> 344 us (0.42)
  matrix products: 412 us -> 0 us
  Pallas kernels: 0 us -> 320 us
  waiting for transfers between devices: 227 us -> 0 us
  other arithmetic: 150 us -> 1.29 us
  between operations: 14.6 us -> 0.66 us
  local copies, waits for them, and re-layouts: 14 us -> 22.5 us
    dot_general x16 -> x0, matrix products: 412 us -> none  [the longest x1 59.3 us: device_step(): lax.dot_general(grad_y, w_down, CONTRACT_COLS, preferred_element_type=jnp...]
    pallas_call x0 -> x1, Pallas kernels: none -> 320 us  [device_step(): pl.pallas_call(functools.partial(layer_kernel, (T, D, F, H, C)), name='la...]
    psum x1 -> x0, waiting for transfers between devices: 227 us -> none  [device_step(): lax.psum(part_sum.astype(jnp.bfloat16), 'model').astype(jnp.float32)]
    convert_element_type x4 -> x0, other arithmetic: 96.6 us -> none  [the longest x1 53.5 us: attention_pair(): (attn_probs * (d_probs - row_delta) * att_scale).astype(jnp.bfloat16)]
    reduce_sum x2 -> x0, other arithmetic: 37.9 us -> none  [the longest x1 21.8 us: attention_pair(): attn_probs = jax.nn.softmax(jnp.where(causal, scores, -1e+30), axis=-1)]
    unnamed x38 -> x13, local copies, waits for them, and re-layouts: 1.38 us -> 22.5 us
    another operation x4 -> x0, other arithmetic: 11.9 us -> none  [the longest x3 7.7 us: device_step(): jnp.stack([rotate(d_q_rot, rope_cos, -rope_sin), rotate(d_k_rot, rope_cos...]
  transfers between devices with their start and end apart: 1 -> 0, of which waited for: 1 -> 0; matrix products, arithmetic and copies ran while one was open for 13% -> 0% of each run, Pallas kernels for 0% -> 0%
where the time goes in v1:
time: 344 us
  Pallas kernels  320 us (93%)
  local copies, waits for them, and re-layouts  22.5 us (7%)
    pallas_call x1, Pallas kernels, device_step(): pl.pallas_call(functools.partial(layer_kernel, (T, D, F, H, C)), name='la...  320 us
    unnamed x13, local copies, waits for them, and re-layouts  22.5 us

profile of v1, /device:TPU:0, one launch (start us, length us, event | category | flops | bytes accessed | tf_op | source)
XLA Modules:
  0.0 344.2 jit_solution(9375397084113829219)
XLA Ops:
  0.6 1.3 reshape.25
  1.9 319.7 %layer_backward.1 = (bf16[4096,2048]{1,0:T(8,128)(2,1)}, bf16[2048,768]{1,0:T(8,128)(2,1)}, bf16[256,2048]{1,0:T(8,128)(2,1)}, bf16[2048,1024]{1,0:T(8,128)(2,1)...) custom-call(bf16[4096,2048]{1,0:T(8,128)(2,1)} %x_hbm.1, ...), custom_call_target="tpu_custom_call" | custom-call | tf_op jit(solution)/shard_map/layer_backward/pallas_call | solution.py:539
  321.6 0.0 copy-start.2
  321.7 14.5 %copy.21 = bf16[4096,2048]{1,0:T(8,128)(2,1)} copy(bf16[4096,2048]{1,0:T(8,128)(2,1)} %get-tuple-element.20) | data formatting | bytes 33554432
  336.1 0.0 copy-done.2
  336.1 0.0 copy-start.3
  336.1 0.0 copy-start.1
  336.1 1.7 copy.22
  337.8 0.3 copy-done.3
  338.0 0.0 copy-start
  338.0 1.0 copy.23
  339.0 1.1 copy-done.1
  340.1 2.0 copy.24
  342.1 0.0 copy-done
  342.2 2.0 copy.25
Async XLA Ops:
  321.6 14.5 %copy-start.2 = (bf16[2048,768]{1,0:T(8,128)(2,1)S(1)}, bf16[2048,768]{1,0:T(8,128)(2,1)}, u32[]{:S(2)}) copy-start(bf16[2048,768]{1,0:T(8,128)(2,1)} %get-tuple-element.21) | copy-start | bytes 9437188
  336.1 1.9 copy-start.3
  336.1 4.0 %copy-start.1 = (bf16[2048,1024]{1,0:T(8,128)(2,1)S(1)}, bf16[2048,1024]{1,0:T(8,128)(2,1)}, u32[]{:S(2)}) copy-start(bf16[2048,1024]{1,0:T(8,128)(2,1)} %get-tuple-element.23) | copy-start | bytes 12582916
  338.0 4.1 %copy-start = (bf16[1024,2048]{1,0:T(8,128)(2,1)S(1)}, bf16[1024,2048]{1,0:T(8,128)(2,1)}, u32[]{:S(2)}) copy-start(bf16[1024,2048]{1,0:T(8,128)(2,1)} %get-tuple-element.24) | copy-start | bytes 12582916

commit v2 on v1

--- a/solution.py
+++ b/solution.py
@@ -30,14 +30,16 @@
     return jnp.minimum(jnp.maximum(v, 0), hi)
 
 
-def layer_kernel(dims, x_hbm, dy_hbm, g_ref, cb_ref, sb_ref, co_ref, so_ref, wqkv_hbm, wo_hbm, w1_hbm, w2_hbm,
+def layer_kernel(dims, plan, x_hbm, dy_hbm, g_ref, mean_ref, rstd_ref, cb_ref, sb_ref, co_ref, so_ref, wqkv_hbm, wo_hbm, w1_hbm, w2_hbm,
                  dx_hbm, dwqkv_hbm, dwo_hbm, dw1_hbm, dw2_hbm, n_hbm, g_hbm, da_hbm, dqkv_hbm, o_hbm, zin_hbm, xin_hbm,
                  qbuf, pst, sib_in, zst, xst, lx, ly,
                  sib_s, sib_r, qs_s, z_r, x_r, dxl_s, dxs_s, dxo_s, dxo_r, dxs_r, st_sem, in_sem, w_sem, out_sem, t2_sem):
     T, D, F, H, C = dims
     R = ROWS
     HALF = R // 2
+    PART = HALF // 2
     NB = T // R
+    NS = 2 * NB
     QPC = C // R
     me = lax.axis_index("model")
     core = lax.rem(me, 2)
@@ -63,7 +65,7 @@
         pl.semaphore_wait(barrier, 2)
 
     def rows_of(t, c):
-        return pl.ds(pl.multiple_of((NB - 1 - t) * R + c * HALF, HALF), HALF)
+        return pl.ds(pl.multiple_of((NB - 1 - t // 2) * R + c * HALF + lax.rem(t, 2) * PART, PART), PART)
 
     def sib_copy(t):
         s = lax.rem(t, 2)
@@ -109,12 +111,13 @@
         cp = sib_copy(t)
         cp.wait_send()
         cp.wait_recv()
-        own = pst[pl.ds(pl.multiple_of(core * HALF, HALF), HALF), :].astype(F32)
-        qbuf[t] = (own + sib_in[lax.rem(t, 2)].astype(F32)).astype(BF16)
-
-        @pl.when(is_out)
-        def _():
-            q_copy(t).start()
+        for h in range(2):
+            own = pst[pl.ds(pl.multiple_of(core * HALF + h * PART, PART), PART), :].astype(F32)
+            qbuf[2 * t + h] = (own + sib_in[lax.rem(t, 2), h * PART:(h + 1) * PART, :].astype(F32)).astype(BF16)
+
+            @pl.when(is_out)
+            def _(h=h):
+                q_copy(2 * t + h).start()
 
     def e3_fetch(t):
         q_copy(t).wait_recv()
@@ -136,11 +139,8 @@
         lx_load(t).wait()
         ly_load(t).wait()
         x_copy(t).wait_send()
-        xv = lx[...].astype(F32)
-        mean = jnp.sum(xv, axis=1, keepdims=True) * (1.0 / D)
-        xc = xv - mean
-        rstd = lax.rsqrt(jnp.sum(xc * xc, axis=1, keepdims=True) * (1.0 / D) + 1e-5)
-        xh = xc * rstd
+        mean, rstd = row_stats(NB - 1 - t // 2, core * 2 + lax.rem(t, 2))
+        xh = (lx[...].astype(F32) - mean) * rstd
         d = (qbuf[t].astype(F32) + xst[...].astype(F32)) * g_ref[...]
         md = jnp.sum(d, axis=1, keepdims=True) * (1.0 / D)
         mdx = jnp.sum(d * xh, axis=1, keepdims=True) * (1.0 / D)
@@ -153,41 +153,59 @@
         dx_out(t).wait_recv()
         dx_fwd(t).start()
 
-    def service_fetch(lo3, hi3, lo4, hi4, lo5, hi5):
-        @pl.when(is_mid & (hi3 > lo3))
+    def lookup(table, k):
+        v = jnp.int32(table[0])
+        for at in range(1, len(table)):
+            v = jnp.where(k == at, table[at], v)
+        return v
+
+    def service_points(table, k):
+        start, fire = lookup(table[0], k), lookup(table[1], k)
+        c = [start % 64, (start // 64) % 64, (start // 4096) % 64]
+        pend = [(start // 262144) % 2, (start // 524288) % 2]
+        points = []
+        for p in range(table[2]):
+            f = [(fire // 2 ** (3 * p + step)) % 2 for step in range(3)]
+            points.append((list(c), list(pend), f))
+            c = [a + b for a, b in zip(c, f)]
+            pend = f[:2]
+        return points
+
+    def service(point):
+        c, pend, f = point
+
+        @pl.when(is_mid & (pend[0] > 0))
         def _():
-            e3_fetch(lo3)
-
-        @pl.when(is_mid & (hi4 > lo4))
+            e3_process(c[0] - 1)
+
+        @pl.when(is_mid & (f[0] > 0))
         def _():
-            e4_fetch(lo4)
-
-        @pl.when(is_out & (hi5 > lo5))
+            e3_fetch(c[0])
+
+        @pl.when(is_mid & (pend[1] > 0))
         def _():
-            e5(lo5)
-
-    def service_process(lo3, hi3, lo4, hi4, lo5, hi5):
-        @pl.when(is_mid & (hi3 > lo3))
+            e4_process(c[1] - 1)
+
+        @pl.when(is_mid & (f[1] > 0))
         def _():
-            e3_process(lo3)
-
-        @pl.when(is_mid & (hi4 > lo4))
+            e4_fetch(c[1])
+
+        @pl.when(is_out & (f[2] > 0))
         def _():
-            e4_process(lo4)
-
-    def n_phase1(u, lag):
-        return clip((5 * (u - lag) + 5) // 6, NB)
-
-    LAG3, LAG4, LAG5 = 2, 4, 6
-
-    def ticks1(u):
-        return (n_phase1(u - 1, LAG3), n_phase1(u, LAG3), n_phase1(u - 1, LAG4), n_phase1(u, LAG4), n_phase1(u - 1, LAG5), n_phase1(u, LAG5))
-
-    def n_phase2(w, lag):
-        return jnp.minimum(n_phase1(NB - 1, lag) + (2 * (w + 1)) // 5, NB)
-
-    def ticks2(w):
-        return (n_phase2(w - 1, LAG3), n_phase2(w, LAG3), n_phase2(w - 1, LAG4), n_phase2(w, LAG4), n_phase2(w - 1, LAG5), n_phase2(w, LAG5))
+            e5(c[2])
+
+    def row_stats(i, part=None):
+        out = []
+        for ref in (mean_ref, rstd_ref):
+            row = ref[pl.ds(i, 1), :]
+            if part is None:
+                col = jnp.broadcast_to(row, (128, R)).T
+            else:
+                row = jnp.where(part >= 2, row[:, HALF:], row[:, :HALF])
+                col = jnp.broadcast_to(row, (128, HALF)).T
+                col = jnp.where(lax.rem(part, 2) == 0, col[:PART], col[PART:])
+            out.append(jnp.concatenate([col] * (D // 128), axis=1))
+        return out
 
     def rope_of(i):
         cb, sb = cb_ref[pl.ds(i, 1), :], sb_ref[pl.ds(i, 1), :]
@@ -207,10 +225,16 @@
             return pl.ds(pl.multiple_of(i * R, R), R)
 
         def x_in(b):
-            return pltpu.make_async_copy(x_hbm.at[blk(b)], ybuf.at[lax.rem(b, 2)], in_sem.at[0, lax.rem(b, 2)])
+            return pltpu.make_async_copy(x_hbm.at[blk(b)], ybuf.at[lax.rem(b + 1, 2)], in_sem.at[0, lax.rem(b + 1, 2)])
 
         def n_out(b):
-            return pltpu.make_async_copy(nbuf.at[lax.rem(b, 2)], n_hbm.at[blk(b)], out_sem.at[0, lax.rem(b, 2)])
+            return pltpu.make_async_copy(nbuf.at[lax.rem(b + 1, 2)], n_hbm.at[blk(b)], out_sem.at[0, lax.rem(b + 1, 2)])
+
+        def n_in(t):
+            return pltpu.make_async_copy(n_hbm.at[blk(NB - 1 - t)], nbuf.at[lax.rem(t, 2)], in_sem.at[1, lax.rem(t, 2)])
+
+        def y_in(t):
+            return pltpu.make_async_copy(dy_hbm.at[blk(NB - 1 - t)], ybuf.at[lax.rem(t + 1, 2)], in_sem.at[0, lax.rem(t + 1, 2)])
 
         w_loads[0].start()
         x_in(0).start()
@@ -218,28 +242,14 @@
             w.start()
         dk[...] = jnp.zeros_like(dk)
         dv[...] = jnp.zeros_like(dv)
-        w_loads[0].wait()
-
-        @pl.loop(0, NB)
-        def _(b):
-            slot = lax.rem(b, 2)
-            x_in(b).wait()
-
-            @pl.when(b + 1 < NB)
-            def _():
-                x_in(b + 1).start()
-
-            @pl.when(b >= 2)
-            def _():
-                n_out(b - 2).wait()
-
-            xv = ybuf[slot].astype(F32)
-            mean = jnp.sum(xv, axis=1, keepdims=True) * (1.0 / D)
-            xc = xv - mean
-            rstd = lax.rsqrt(jnp.sum(xc * xc, axis=1, keepdims=True) * (1.0 / D) + 1e-5)
-            nbuf[slot] = ((xc * rstd) * g_ref[...]).astype(BF16)
-            n_out(b).start()
-            kvp = mm(nbuf[slot], wqkv[:, H:])
+
+        def normed(b):
+            slot = lax.rem(b + 1, 2)
+            mean, rstd = row_stats(b)
+            nbuf[slot] = (((ybuf[slot].astype(F32) - mean) * rstd) * g_ref[...]).astype(BF16)
+
+        def keys_values(b):
+            kvp = mm(nbuf[lax.rem(b + 1, 2)], wqkv[:, H:])
             cosf, sinf = rope_of(b)
             kf = rope(kvp[:, :H], cosf, sinf)
             vf = kvp[:, H:]
@@ -248,14 +258,35 @@
             kT[:, blk(b)] = kf.T.astype(BF16)
             vT[:, blk(b)] = vf.T.astype(BF16)
 
+        x_in(1).start()
+        x_in(0).wait()
+        normed(0)
+        n_out(0).start()
+        w_loads[0].wait()
+
+        @pl.loop(0, NB - 1)
+        def _(b):
+            x_in(b + 1).wait()
+
+            @pl.when(b + 2 < NB)
+            def _():
+                x_in(b + 2).start()
+
+            @pl.when(b + 2 == NB)
+            def _():
+                y_in(0).start()
+
+            @pl.when(b >= 1)
+            def _():
+                n_out(b - 1).wait()
+
+            normed(b + 1)
+            keys_values(b)
+            n_out(b + 1).start()
+
+        keys_values(NB - 1)
         n_out(NB - 2).wait()
         n_out(NB - 1).wait()
-
-        def n_in(t):
-            return pltpu.make_async_copy(n_hbm.at[blk(NB - 1 - t)], nbuf.at[lax.rem(t, 2)], in_sem.at[1, lax.rem(t, 2)])
-
-        def y_in(t):
-            return pltpu.make_async_copy(dy_hbm.at[blk(NB - 1 - t)], ybuf.at[lax.rem(t, 2)], in_sem.at[0, lax.rem(t, 2)])
 
         def outs(t):
             s, i = lax.rem(t, 2), NB - 1 - t
@@ -264,8 +295,6 @@
                     pltpu.make_async_copy(dqkvst.at[s], dqkv_hbm.at[blk(i)], out_sem.at[2, s]),
                     pltpu.make_async_copy(ost.at[s], o_hbm.at[blk(i)], out_sem.at[3, s])]
 
-        n_in(0).start()
-        y_in(0).start()
         for w in w_loads[1:]:
             w.wait()
 
@@ -273,44 +302,52 @@
         def _(t):
             slot = lax.rem(t, 2)
             i = NB - 1 - t
-            n_in(t).wait()
-            y_in(t).wait()
-
-            @pl.when(t + 1 < NB)
-            def _():
-                n_in(t + 1).start()
-                y_in(t + 1).start()
+            yslot = lax.rem(t + 1, 2)
 
             @pl.when(t >= 2)
             def _():
+                n_in(t).wait()
                 for cp in outs(t - 2):
                     cp.wait()
 
-            service_fetch(*ticks1(t))
+            y_in(t).wait()
+
+            @pl.when((t >= 1) & (t + 1 < NB))
+            def _():
+                n_in(t + 1).start()
+
+            @pl.when(t + 1 < NB)
+            def _():
+                y_in(t + 1).start()
+
+            points = service_points(plan[0], t)
+            service(points[0])
 
             FT = min(512, F)
             for f in range(0, F, FT):
                 a = mm(nbuf[slot], w1[:, f:f + FT])
-                da = mm_nt(ybuf[slot], w2[f:f + FT, :])
+                da = mm_nt(ybuf[yslot], w2[f:f + FT, :])
                 phi = 0.5 + 0.5 * lax.erf(a * 0.7071067811865476)
                 gst[slot, :, f:f + FT] = (a * phi).astype(BF16)
                 dast[slot, :, f:f + FT] = (da * (phi + a * (0.3989422804014327 * jnp.exp(-0.5 * (a * a))))).astype(BF16)
-            for cp in outs(t)[:2]:
-                cp.start()
-
-            @pl.when(t > 0)
-            def _():
-                pair_sum(t - 1)
-
-            service_process(*ticks1(t))
 
             cosf, sinf = rope_of(i)
             qf = rope(mm(nbuf[slot], wqkv[:, :H]), cosf, sinf).astype(BF16).astype(F32) * (H ** -0.5)
             qs[...] = qf.astype(BF16)
             qT[...] = qf.T.astype(BF16)
-            dof = mm_nt(ybuf[slot], wo[...])
+            dof = mm_nt(ybuf[yslot], wo[...])
             do[...] = dof.astype(BF16)
             doT[...] = dof.T.astype(BF16)
+            g_out, da_out, dqkv_out, o_out = outs(t)
+            g_out.start()
+            da_out.start()
+
+            @pl.when(t > 0)
+            def _():
+                pair_sum(t - 1)
+
+            service(points[1])
+
             nfull = i // QPC
 
             def chunk(j):
@@ -318,23 +355,27 @@
 
             def pass_a(j, carry, masked):
                 m, l, dl = carry
-                st = mm(kv[chunk(j), :], qT[...])
-                if masked:
-                    key = j * C + lax.broadcasted_iota(jnp.int32, st.shape, 0)
-                    query = i * R + lax.broadcasted_iota(jnp.int32, st.shape, 1)
-                    st = jnp.where(key <= query, st, NEG)
-                dp = mm(vv[chunk(j), :], doT[...])
-                m_new = jnp.maximum(m, jnp.max(st, axis=0, keepdims=True))
-                alpha = jnp.exp(m - m_new)
-                e = jnp.exp(st - m_new)
-                es[chunk(j), :] = e
-                dps[chunk(j), :] = dp
-                msc[pl.ds(j, 1), :] = m_new
-                return m_new, l * alpha + jnp.sum(e, axis=0, keepdims=True), dl * alpha + jnp.sum(e * dp, axis=0, keepdims=True)
+                for u in range(QPC):
+                    keys = pl.ds(pl.multiple_of(j * C + u * R, R), R)
+                    st = mm(kv[keys, :], qT[...])
+                    if masked:
+                        key = j * C + u * R + lax.broadcasted_iota(jnp.int32, st.shape, 0)
+                        query = i * R + lax.broadcasted_iota(jnp.int32, st.shape, 1)
+                        st = jnp.where(key <= query, st, NEG)
+                    dp = mm(vv[keys, :], doT[...])
+                    m_new = jnp.maximum(m, jnp.max(st, axis=0, keepdims=True))
+                    alpha = jnp.exp(m - m_new)
+                    e = jnp.exp(st - m_new)
+                    es[keys, :] = e
+                    dps[keys, :] = dp
+                    msc[pl.ds(j * QPC + u, 1), :] = m_new
+                    m, l, dl = m_new, l * alpha + jnp.sum(e, axis=0, keepdims=True), dl * alpha + jnp.sum(e * dp, axis=0, keepdims=True)
+                return m, l, dl
 
             init = (jnp.full((1, R), NEG, F32), jnp.zeros((1, R), F32), jnp.zeros((1, R), F32))
             carry = lax.fori_loop(0, nfull, functools.partial(pass_a, masked=False), init)
             m, l, dl = pass_a(nfull, carry, True)
+            service(points[2])
             inv_l = 1.0 / l
             delta = dl * inv_l
             oT[...] = jnp.zeros_like(oT)
@@ -342,23 +383,35 @@
 
             @pl.loop(0, nfull + 1)
             def _(j):
-                p = es[chunk(j), :] * (jnp.exp(msc[pl.ds(j, 1), :] - m) * inv_l)
-                pb = p.astype(BF16)
-                ds = (p * (dps[chunk(j), :] - delta)).astype(BF16)
+                pbs, dss = [], []
+                for u in range(QPC):
+                    keys = pl.ds(pl.multiple_of(j * C + u * R, R), R)
+                    p = es[keys, :] * (jnp.exp(msc[pl.ds(j * QPC + u, 1), :] - m) * inv_l)
+                    pbs.append(p.astype(BF16))
+                    dss.append((p * (dps[keys, :] - delta)).astype(BF16))
+                pb, ds = jnp.concatenate(pbs, axis=0), jnp.concatenate(dss, axis=0)
                 oT[...] += mm(vT[:, chunk(j)], pb)
                 dqT[...] += mm(kT[:, chunk(j)], ds)
                 dv[chunk(j), :] += mm(pb, do[...])
                 dk[chunk(j), :] += mm(ds, qs[...])
 
+            service(points[3])
+
+            EARLY = min(4 * R, T, D)
+            for c in range(0, EARLY, R):
+                es[c:c + R, :] = mm_nt(dast[slot], w1[c:c + R, :])
+
             ost[slot] = oT[...].T.astype(BF16)
             dqkvst[slot, :, :H] = rope(dqT[...].T * (H ** -0.5), cosf, -sinf).astype(BF16)
             dqkvst[slot, :, H:2 * H] = rope(dk[blk(i), :], cosf, -sinf).astype(BF16)
             dqkvst[slot, :, 2 * H:] = dv[blk(i), :].astype(BF16)
-            for cp in outs(t)[2:]:
-                cp.start()
+            dqkv_out.start()
+            o_out.start()
 
             DT = min(512, D)
-            for c in range(0, D, DT):
+            for c in range(0, EARLY, R):
+                pst[:, c:c + R] = (es[c:c + R, :] + mm_nt(dqkvst[slot], wqkv[c:c + R, :])).astype(BF16)
+            for c in range(EARLY, D, DT):
                 pst[:, c:c + DT] = (mm_nt(dast[slot], w1[c:c + DT, :]) + mm_nt(dqkvst[slot], wqkv[c:c + DT, :])).astype(BF16)
             sib_copy(t).start()
 
@@ -374,7 +427,7 @@
         pltpu.VMEM((2, R, D), BF16), pltpu.VMEM((2, R, D), BF16), pltpu.VMEM((2, R, F), BF16), pltpu.VMEM((2, R, F), BF16),
         pltpu.VMEM((2, R, 3 * H), BF16), pltpu.VMEM((2, R, H), BF16),
         pltpu.VMEM((R, H), BF16), pltpu.VMEM((H, R), BF16), pltpu.VMEM((R, H), BF16), pltpu.VMEM((H, R), BF16),
-        pltpu.VMEM((H, R), F32), pltpu.VMEM((H, R), F32), pltpu.VMEM((8, R), F32))
+        pltpu.VMEM((H, R), F32), pltpu.VMEM((H, R), F32), pltpu.VMEM((max(8, NB), R), F32))
 
     NT1, NT2 = D // H, F // H
 
@@ -404,13 +457,11 @@
         def out3():
             return pltpu.make_async_copy(w2st.at[NT2 % 2], dwo_hbm, t2_sem.at[1, NT2 % 2])
 
-        loads[0].start()
         nt_in(0).start()
         loads[1].start()
+        loads[0].start()
         loads[2].start()
         pair_sum(NB - 1)
-        loads[0].wait()
-        loads[1].wait()
 
         @pl.loop(0, NT1)
         def _(m):
@@ -430,12 +481,23 @@
                 for cp in out1(m - 2):
                     cp.wait()
 
-            service_fetch(*ticks2(m))
+            points = service_points(plan[1], m)
+            service(points[0])
+
+            @pl.when(m == 0)
+            def _():
+                loads[1].wait()
+
+            wqst[s] = mm_tn(nt[s], dqkv[...]).astype(BF16)
+            service(points[1])
+
+            @pl.when(m == 0)
+            def _():
+                loads[0].wait()
+
             w1st[s] = mm_tn(nt[s], da[...]).astype(BF16)
-            wqst[s] = mm_tn(nt[s], dqkv[...]).astype(BF16)
             for cp in out1(m):
                 cp.start()
-            service_process(*ticks2(m))
 
         for m in (NT1 - 2, NT1 - 1):
             for cp in out1(m):
@@ -459,17 +521,21 @@
             def _():
                 out2(m - 2).wait()
 
-            service_fetch(*ticks2(NT1 + m))
-            w2st[s] = mm_tn(nt[s], dy[...]).astype(BF16)
+            points = service_points(plan[1], NT1 + m)
+            service(points[0])
+            w2st[s, :, :D // 2] = mm_tn(nt[s], dy[:, :D // 2]).astype(BF16)
+            service(points[1])
+            w2st[s, :, D // 2:] = mm_tn(nt[s], dy[:, D // 2:]).astype(BF16)
             out2(m).start()
-            service_process(*ticks2(NT1 + m))
 
         o_in().wait()
         out2(NT2 - 2).wait()
-        service_fetch(*ticks2(NT1 + NT2))
-        w2st[NT2 % 2] = mm_tn(nt[NT2 % 2], dy[...]).astype(BF16)
+        points = service_points(plan[1], NT1 + NT2)
+        service(points[0])
+        w2st[NT2 % 2, :, :D // 2] = mm_tn(nt[NT2 % 2], dy[:, :D // 2]).astype(BF16)
+        service(points[1])
+        w2st[NT2 % 2, :, D // 2:] = mm_tn(nt[NT2 % 2], dy[:, D // 2:]).astype(BF16)
         out3().start()
-        service_process(*ticks2(NT1 + NT2))
         out2(NT2 - 1).wait()
         out3().wait()
 
@@ -478,14 +544,14 @@
         pltpu.VMEM((T, F), BF16), pltpu.VMEM((T, 3 * H), BF16), pltpu.VMEM((T, D), BF16), pltpu.VMEM((2, T, H), BF16),
         pltpu.VMEM((2, H, F), BF16), pltpu.VMEM((2, H, 3 * H), BF16), pltpu.VMEM((2, H, D), BF16))
 
-    WL = NT1 + NT2
-    l3, l4, l5 = n_phase2(WL, LAG3), n_phase2(WL, LAG4), n_phase2(WL, LAG5)
+    (l3, l4, l5), last3, last4 = plan[2]
+    service(([l3, l4, l5], [jnp.int32(last3), jnp.int32(last4)], [jnp.int32(0)] * 3))
 
     @pl.when(is_mid)
     def _():
-        @pl.loop(0, NB - l4)
+        @pl.loop(0, NS - l4)
         def _(k):
-            @pl.when(l3 + k < NB)
+            @pl.when(l3 + k < NS)
             def _():
                 e3_fetch(l3 + k)
                 e3_process(l3 + k)
@@ -493,7 +559,7 @@
             e4_fetch(l4 + k)
             e4_process(l4 + k)
 
-        @pl.loop(0, NB)
+        @pl.loop(0, NS)
         def _(t):
             dx_local(t).wait()
             dx_sib(t).wait_send()
@@ -502,15 +568,94 @@
 
     @pl.when(is_out)
     def _():
-        @pl.loop(l5, NB)
+        @pl.loop(l5, NS)
         def _(t):
             e5(t)
 
-        @pl.loop(0, NB)
+        @pl.loop(0, NS)
         def _(t):
             q_copy(t).wait_send()
             dx_fwd(t).wait_send()
             dx_fwd(t).wait_recv()
+
+
+def service_plan(blocks, tiles, keys_per_chunk):
+    wire, lat, slow, count = 5.65, 2.5, 1.08, 2 * blocks
+    at, ready, now = [], [], 14.0
+    for t in range(blocks):
+        chunks = (blocks - 1 - t) * ROWS // keys_per_chunk + 1
+        mlp = now + 3.2 * slow
+        at += [now, mlp, mlp + 0.56 * chunks * slow, mlp + 1.28 * chunks * slow]
+        if t:
+            ready += [mlp, mlp]
+        now = at[-1] + 2.3 * slow
+    ready += [now + 0.5, now + 0.5]
+    now += 2.0
+    for m in range(tiles):
+        at += [now, now + 2.1 * slow]
+        now += 4.3 * slow
+    at.append(now)
+    fires = []
+    for step in range(3):
+        table, sent, free, k = [], [], 0.0, 0
+        for t in range(count):
+            free = max(free, ready[t]) + wire
+            while k < len(at) - 1 and at[k] < free + lat:
+                k += 1
+            if k < len(at) - 1:
+                table.append(k)
+                sent.append(at[k + 1])
+                k += 1
+            else:
+                sent.append(free + lat)
+        fires.append(set(table))
+        ready = sent
+    done, last, tables = [0, 0, 0], [0, 0], []
+    k = 0
+    for units, points in ((blocks, 4), (tiles, 2)):
+        starts, codes = [], []
+        for _ in range(units):
+            starts.append(done[0] + 64 * done[1] + 4096 * done[2] + 262144 * last[0] + 524288 * last[1])
+            code = 0
+            for p in range(points):
+                f = [int(k in fire) for fire in fires]
+                code += sum(v * 2 ** (3 * p + step) for step, v in enumerate(f))
+                done = [a + b for a, b in zip(done, f)]
+                last = f[:2]
+                k += 1
+            codes.append(code)
+        tables.append((tuple(starts), tuple(codes), points))
+    return tables[0], tables[1], (tuple(done), last[0], last[1])
+
+
+def copy_kernel(*refs):
+    n = len(refs) // 4
+    pieces = []
+    for src, dst, buf, sem in zip(refs[:n], refs[n:2 * n], refs[2 * n:3 * n], refs[3 * n:]):
+        count = sem.shape[1]
+        rows = src.shape[0] // count
+        for p in range(count):
+            part = pl.ds(p * rows, rows)
+            pieces.append((pltpu.make_async_copy(src.at[part], buf.at[part], sem.at[0, p]), pltpu.make_async_copy(buf.at[part], dst.at[part], sem.at[1, p])))
+    for load, _ in pieces:
+        load.start()
+    for load, store in pieces:
+        load.wait()
+        store.start()
+    for _, store in pieces:
+        store.wait()
+
+
+def copy_out(arrays):
+    any_spec = pl.BlockSpec(memory_space=pl.ANY)
+    counts = [2 ** max(0, (a.size // (512 * 1024)).bit_length() - 1) for a in arrays]
+    size = sum(a.size * 2 for a in arrays)
+    return pl.pallas_call(
+        copy_kernel, name="results",
+        out_shape=[jax.ShapeDtypeStruct(a.shape, a.dtype) for a in arrays],
+        in_specs=[any_spec] * len(arrays), out_specs=[any_spec] * len(arrays),
+        scratch_shapes=[pltpu.VMEM(a.shape, a.dtype) for a in arrays] + [pltpu.SemaphoreType.DMA((2, c)) for c in counts],
+        compiler_params=pltpu.CompilerParams(vmem_limit_bytes=size + (4 << 20)))(*arrays)
 
 
 def rope_tables(blocks, head_dim):
@@ -537,22 +682,22 @@
         vmem = pl.BlockSpec(memory_space=pltpu.VMEM)
         sds = lambda *s: jax.ShapeDtypeStruct(s, BF16)
         outs = pl.pallas_call(
-            functools.partial(layer_kernel, (T, D, F, H, C)),
+            functools.partial(layer_kernel, (T, D, F, H, C), service_plan(NB, D // H + F // H + 1, C)),
             name="layer_backward",
             out_shape=[sds(T, D), sds(D, 3 * H), sds(H, D), sds(D, F), sds(F, D),
-                       sds(T, D), sds(T, F), sds(T, F), sds(T, 3 * H), sds(T, H), sds(NB, HALF, D), sds(NB, HALF, D)],
-            in_specs=[any_spec, any_spec, vmem, vmem, vmem, vmem, vmem, any_spec, any_spec, any_spec, any_spec],
+                       sds(T, D), sds(T, F), sds(T, F), sds(T, 3 * H), sds(T, H), sds(2 * NB, HALF // 2, D), sds(2 * NB, HALF // 2, D)],
+            in_specs=[any_spec, any_spec] + [vmem] * 7 + [any_spec, any_spec, any_spec, any_spec],
             out_specs=[any_spec] * 12,
             scratch_shapes=[
-                pltpu.VMEM((NB, HALF, D), BF16), pltpu.VMEM((ROWS, D), BF16), pltpu.VMEM((2, HALF, D), BF16),
-                pltpu.VMEM((HALF, D), BF16), pltpu.VMEM((HALF, D), BF16), pltpu.VMEM((HALF, D), BF16), pltpu.VMEM((HALF, D), BF16),
+                pltpu.VMEM((2 * NB, HALF // 2, D), BF16), pltpu.VMEM((ROWS, D), BF16), pltpu.VMEM((2, HALF, D), BF16),
+                *[pltpu.VMEM((HALF // 2, D), BF16)] * 4,
                 pltpu.SemaphoreType.DMA((2,)), pltpu.SemaphoreType.DMA((2,))]
-            + [pltpu.SemaphoreType.DMA((NB,))] * 8
+            + [pltpu.SemaphoreType.DMA((2 * NB,))] * 8
             + [pltpu.SemaphoreType.DMA((4,)), pltpu.SemaphoreType.DMA((2, 2)), pltpu.SemaphoreType.DMA((4,)), pltpu.SemaphoreType.DMA((4, 2)),
                pltpu.SemaphoreType.DMA((3, 2))],
             compiler_params=pltpu.CompilerParams(collective_id=0, has_side_effects=True, vmem_limit_bytes=67043328),
-        )(resid_x, grad_y, ln_gain.astype(F32).reshape(1, D), *tabs, w_qkv, w_out.reshape(H, D), w_up, w_down)
-        grad_x, grad_w_qkv, grad_w_out, grad_w_up, grad_w_down = outs[:5]
+        )(resid_x, grad_y, ln_gain.astype(F32).reshape(1, D), ln_mean.reshape(NB, ROWS), ln_rstd.reshape(NB, ROWS), *tabs, w_qkv, w_out.reshape(H, D), w_up, w_down)
+        grad_x, grad_w_qkv, grad_w_out, grad_w_up, grad_w_down = copy_out(outs[:5])
         return grad_x, grad_w_qkv, grad_w_out.reshape(1, H, D), grad_w_up, grad_w_down
 
     in_specs = (P("data", None), P("data"), P("data"), P(None), P("data", None), P(None, "model"), P("model", None, None), P(None, "model"), P("model", None))

time: 344 us -> 310 us (0.901)
  Pallas kernels: 320 us -> 297 us
  local copies, waits for them, and re-layouts: 22.5 us -> 10.1 us
    pallas_call x1 -> x2, Pallas kernels: 320 us -> 297 us  [the longest x1 281 us: device_step(): pl.pallas_call(functools.partial(layer_kernel, (T, D, F, H, C), service_p...]
    unnamed x13 -> x8, local copies, waits for them, and re-layouts: 22.5 us -> 7.48 us
where the time goes in v2:
time: 310 us; the launch traced here: 309 us
  Pallas kernels  297 us (96%)
  local copies, waits for them, and re-layouts  10.1 us (3%)
    pallas_call x1, Pallas kernels, device_step(): pl.pallas_call(functools.partial(layer_kernel, (T, D, F, H, C), service_p...  281 us
    pallas_call x1, Pallas kernels, copy_out(): pl.pallas_call(copy_kernel, name='results', out_shape=[jax.ShapeDtypeStru...  16 us
    unnamed x8, local copies, waits for them, and re-layouts  7.48 us

profile of v2, /device:TPU:0, one launch (start us, length us, event | category | flops | bytes accessed | tf_op | source)
XLA Modules:
  0.0 309.1 jit_solution(8403262557358220300)
XLA Ops:
  0.6 1.3 reshape.33
  1.9 1.3 reshape.29.mean_ref
  3.2 1.3 reshape.30.rstd_ref
  4.6 280.8 %layer_backward.1 = (bf16[4096,2048]{1,0:T(8,128)(2,1)}, bf16[2048,768]{1,0:T(8,128)(2,1)}, bf16[256,2048]{1,0:T(8,128)(2,1)}, bf16[2048,1024]{1,0:T(8,128)(2,1)...) custom-call(bf16[4096,2048]{1,0:T(8,128)(2,1)} %x_hbm.1, ...), custom_call_target="tpu_custom_call" | custom-call | tf_op jit(solution)/shard_map/layer_backward/pallas_call | solution.py:684
  285.4 0.0 copy-start
  285.4 2.2 copy-done
  287.6 0.0 copy-start.1
  287.6 2.2 copy-done.1
  289.8 0.0 copy-start.2
  289.8 1.9 copy-done.2
  291.7 0.0 copy-start.3
  291.7 1.2 copy-done.3
  292.9 16.0 %results.1 = (bf16[4096,2048]{1,0:T(8,128)(2,1)}, bf16[2048,768]{1,0:T(8,128)(2,1)}, bf16[256,2048]{1,0:T(8,128)(2,1)}, bf16[2048,1024]{1,0:T(8,128)(2,1)}, bf16[1024,2048]{1,0:T(8,128)(2,1)}) custom-call(bf16[4096,2048]{1,0:T(8,128)(2,1)} %get-tuple-element.15.refs_0_, bf16[2048,768]{1,0:T(8,128)(2,1)S(1)} %copy-done.2, bf16[256,2048]{1,0:T(8,128)(2,1)S(1)} %copy-done.3, ...), custom_call_target="tpu_custom_call" | custom-call | tf_op jit(solution)/shard_map/results/pallas_call | solution.py:653
Async XLA Ops:
  285.4 2.2 copy-start
  287.6 2.2 copy-start.1
  289.8 1.9 copy-start.2
  291.7 1.2 copy-start.3

commit v3 on v2

--- a/solution.py
+++ b/solution.py
@@ -30,9 +30,9 @@
     return jnp.minimum(jnp.maximum(v, 0), hi)
 
 
-def layer_kernel(dims, plan, x_hbm, dy_hbm, g_ref, mean_ref, rstd_ref, cb_ref, sb_ref, co_ref, so_ref, wqkv_hbm, wo_hbm, w1_hbm, w2_hbm,
-                 dx_hbm, dwqkv_hbm, dwo_hbm, dw1_hbm, dw2_hbm, n_hbm, g_hbm, da_hbm, dqkv_hbm, o_hbm, zin_hbm, xin_hbm,
-                 qbuf, pst, sib_in, zst, xst, lx, ly,
+def layer_kernel(dims, plan, x_hbm, dy_hbm, small_ref, cb_ref, sb_ref, co_ref, so_ref, wqkv_hbm, wo_hbm, w1_hbm, w2_hbm,
+                 dx_hbm, dwqkv_hbm, dw1_hbm, n_hbm, g_hbm, da_hbm, dqkv_hbm, o_hbm, zin_hbm, xin_hbm,
+                 gain, qbuf, pst, sib_in, zst, xst, lx, ly,
                  sib_s, sib_r, qs_s, z_r, x_r, dxl_s, dxs_s, dxo_s, dxo_r, dxs_r, st_sem, in_sem, w_sem, out_sem, t2_sem):
     T, D, F, H, C = dims
     R = ROWS
@@ -51,6 +51,8 @@
     is_mid = (z == 1) | (z == 2)
     is_out = (z == 0) | (z == 3)
 
+    for c in range(D // R):
+        gain[:, c * R:(c + 1) * R] = small_ref[2 * NB + c:2 * NB + c + 1, :]
     barrier = pltpu.get_barrier_semaphore()
     pl.semaphore_signal(barrier, inc=1, device_id={"model": sibling}, device_id_type=MESH)
     pl.semaphore_signal(barrier, inc=1, device_id={"model": near}, device_id_type=MESH)
@@ -141,7 +143,7 @@
         x_copy(t).wait_send()
         mean, rstd = row_stats(NB - 1 - t // 2, core * 2 + lax.rem(t, 2))
         xh = (lx[...].astype(F32) - mean) * rstd
-        d = (qbuf[t].astype(F32) + xst[...].astype(F32)) * g_ref[...]
+        d = (qbuf[t].astype(F32) + xst[...].astype(F32)) * gain[...]
         md = jnp.sum(d, axis=1, keepdims=True) * (1.0 / D)
         mdx = jnp.sum(d * xh, axis=1, keepdims=True) * (1.0 / D)
         qbuf[t] = (ly[...].astype(F32) + rstd * (d - md - xh * mdx)).astype(BF16)
@@ -196,8 +198,8 @@
 
     def row_stats(i, part=None):
         out = []
-        for ref in (mean_ref, rstd_ref):
-            row = ref[pl.ds(i, 1), :]
+        for first in (0, NB):
+            row = small_ref[pl.ds(first + i, 1), :]
             if part is None:
                 col = jnp.broadcast_to(row, (128, R)).T
             else:
@@ -218,7 +220,7 @@
         other = jnp.where(lane < H // 8, pltpu.roll(x0, 128 - H // 8, 1), pltpu.roll(x0, H // 8, 1))
         return jnp.concatenate([x0 * cosf + other * sinf, x[:, 128:]], axis=1)
 
-    def attention_phase(kv, kT, vv, vT, dk, dv, es, dps, w1, w2, wqkv, wo, nbuf, ybuf, gst, dast, dqkvst, ost, qs, qT, do, doT, oT, dqT, msc):
+    def attention_phase(kv, kT, vv, vT, dk, dv, es, dps, w1, w2, wqkv, wo, nbuf, ybuf, gst, dast, dqkvst, ost, qs, qT, do, doT, oT, dqT, msc, stat):
         w_loads = [pltpu.make_async_copy(s, d_, w_sem.at[k]) for k, (s, d_) in enumerate(((wqkv_hbm, wqkv), (wo_hbm, wo), (w1_hbm, w1), (w2_hbm, w2)))]
 
         def blk(i):
@@ -246,7 +248,7 @@
         def normed(b):
             slot = lax.rem(b + 1, 2)
             mean, rstd = row_stats(b)
-            nbuf[slot] = (((ybuf[slot].astype(F32) - mean) * rstd) * g_ref[...]).astype(BF16)
+            nbuf[slot] = (((ybuf[slot].astype(F32) - mean) * rstd) * gain[...]).astype(BF16)
 
         def keys_values(b):
             kvp = mm(nbuf[lax.rem(b + 1, 2)], wqkv[:, H:])
@@ -350,50 +352,66 @@
 
             nfull = i // QPC
 
-            def chunk(j):
-                return pl.ds(pl.multiple_of(j * C, C), C)
-
-            def pass_a(j, carry, masked):
+            below = jnp.where(lax.broadcasted_iota(jnp.int32, (R, R), 0) <= lax.broadcasted_iota(jnp.int32, (R, R), 1), 0.0, NEG)
+
+            def part(j, u, n=1):
+                return pl.ds(pl.multiple_of(j * C + u * R, R), n * R)
+
+            def pass_a(j, carry, subs, diagonal):
                 m, l, dl = carry
-                for u in range(QPC):
-                    keys = pl.ds(pl.multiple_of(j * C + u * R, R), R)
-                    st = mm(kv[keys, :], qT[...])
-                    if masked:
-                        key = j * C + u * R + lax.broadcasted_iota(jnp.int32, st.shape, 0)
-                        query = i * R + lax.broadcasted_iota(jnp.int32, st.shape, 1)
-                        st = jnp.where(key <= query, st, NEG)
-                    dp = mm(vv[keys, :], doT[...])
+                for u in range(subs):
+                    st = mm(kv[part(j, u), :], qT[...])
+                    if diagonal and u == subs - 1:
+                        st = jnp.where(below == 0.0, st, NEG)
+                    dp = mm(vv[part(j, u), :], doT[...])
                     m_new = jnp.maximum(m, jnp.max(st, axis=0, keepdims=True))
                     alpha = jnp.exp(m - m_new)
                     e = jnp.exp(st - m_new)
-                    es[keys, :] = e
-                    dps[keys, :] = dp
+                    es[part(j, u), :] = e
+                    dps[part(j, u), :] = dp
                     msc[pl.ds(j * QPC + u, 1), :] = m_new
                     m, l, dl = m_new, l * alpha + jnp.sum(e, axis=0, keepdims=True), dl * alpha + jnp.sum(e * dp, axis=0, keepdims=True)
                 return m, l, dl
 
             init = (jnp.full((1, R), NEG, F32), jnp.zeros((1, R), F32), jnp.zeros((1, R), F32))
-            carry = lax.fori_loop(0, nfull, functools.partial(pass_a, masked=False), init)
-            m, l, dl = pass_a(nfull, carry, True)
+            carry = lax.fori_loop(0, nfull, functools.partial(pass_a, subs=QPC, diagonal=False), init)
+            for row, value in enumerate(carry):
+                stat[row:row + 1, :] = value
+            for v in range(QPC):
+                @pl.when(lax.rem(i, QPC) == v)
+                def _(v=v):
+                    carry = pass_a(nfull, tuple(stat[row:row + 1, :] for row in range(3)), v + 1, True)
+                    for row, value in enumerate(carry):
+                        stat[row:row + 1, :] = value
+
             service(points[2])
-            inv_l = 1.0 / l
-            delta = dl * inv_l
+            m = stat[0:1, :]
+            inv_l = 1.0 / stat[1:2, :]
+            delta = stat[2:3, :] * inv_l
             oT[...] = jnp.zeros_like(oT)
             dqT[...] = jnp.zeros_like(dqT)
 
-            @pl.loop(0, nfull + 1)
+            def pass_b(j, subs):
+                pbs, dss = [], []
+                for u in range(subs):
+                    p = es[part(j, u), :] * (jnp.exp(msc[pl.ds(j * QPC + u, 1), :] - m) * inv_l)
+                    pbs.append(p.astype(BF16))
+                    dss.append((p * (dps[part(j, u), :] - delta)).astype(BF16))
+                pb, ds = jnp.concatenate(pbs, axis=0), jnp.concatenate(dss, axis=0)
+                keys = part(j, 0, subs)
+                oT[...] += mm(vT[:, keys], pb)
+                dqT[...] += mm(kT[:, keys], ds)
+                dv[keys, :] += mm(pb, do[...])
+                dk[keys, :] += mm(ds, qs[...])
+
+            @pl.loop(0, nfull)
             def _(j):
-                pbs, dss = [], []
-                for u in range(QPC):
-                    keys = pl.ds(pl.multiple_of(j * C + u * R, R), R)
-                    p = es[keys, :] * (jnp.exp(msc[pl.ds(j * QPC + u, 1), :] - m) * inv_l)
-                    pbs.append(p.astype(BF16))
-                    dss.append((p * (dps[keys, :] - delta)).astype(BF16))
-                pb, ds = jnp.concatenate(pbs, axis=0), jnp.concatenate(dss, axis=0)
-                oT[...] += mm(vT[:, chunk(j)], pb)
-                dqT[...] += mm(kT[:, chunk(j)], ds)
-                dv[chunk(j), :] += mm(pb, do[...])
-                dk[chunk(j), :] += mm(ds, qs[...])
+                pass_b(j, QPC)
+
+            for v in range(QPC):
+                @pl.when(lax.rem(i, QPC) == v)
+                def _(v=v):
+                    pass_b(nfull, v + 1)
 
             service(points[3])
 
@@ -427,40 +445,27 @@
         pltpu.VMEM((2, R, D), BF16), pltpu.VMEM((2, R, D), BF16), pltpu.VMEM((2, R, F), BF16), pltpu.VMEM((2, R, F), BF16),
         pltpu.VMEM((2, R, 3 * H), BF16), pltpu.VMEM((2, R, H), BF16),
         pltpu.VMEM((R, H), BF16), pltpu.VMEM((H, R), BF16), pltpu.VMEM((R, H), BF16), pltpu.VMEM((H, R), BF16),
-        pltpu.VMEM((H, R), F32), pltpu.VMEM((H, R), F32), pltpu.VMEM((max(8, NB), R), F32))
-
-    NT1, NT2 = D // H, F // H
-
-    def weight_phase(da, dqkv, dy, nt, w1st, wqst, w2st):
-        loads = [pltpu.make_async_copy(s, d_, w_sem.at[k]) for k, (s, d_) in enumerate(((da_hbm, da), (dqkv_hbm, dqkv), (dy_hbm, dy)))]
+        pltpu.VMEM((H, R), F32), pltpu.VMEM((H, R), F32), pltpu.VMEM((max(8, NB), R), F32), pltpu.VMEM((8, R), F32))
+
+    NT1 = D // H
+
+    def weight_phase(da, dqkv, nt, w1st, wqst):
+        loads = [pltpu.make_async_copy(s, d_, w_sem.at[k]) for k, (s, d_) in enumerate(((da_hbm, da), (dqkv_hbm, dqkv)))]
 
         def cols(m):
             return pl.ds(pl.multiple_of(m * H, H), H)
 
         def nt_in(m):
             return pltpu.make_async_copy(n_hbm.at[:, cols(m)], nt.at[lax.rem(m, 2)], t2_sem.at[0, lax.rem(m, 2)])
-
-        def g_in(m):
-            return pltpu.make_async_copy(g_hbm.at[:, cols(m)], nt.at[lax.rem(m, 2)], t2_sem.at[0, lax.rem(m, 2)])
-
-        def o_in():
-            return pltpu.make_async_copy(o_hbm, nt.at[NT2 % 2], t2_sem.at[0, NT2 % 2])
 
         def out1(m):
             s = lax.rem(m, 2)
             return [pltpu.make_async_copy(w1st.at[s], dw1_hbm.at[cols(m)], t2_sem.at[1, s]),
                     pltpu.make_async_copy(wqst.at[s], dwqkv_hbm.at[cols(m)], t2_sem.at[2, s])]
 
-        def out2(m):
-            return pltpu.make_async_copy(w2st.at[lax.rem(m, 2)], dw2_hbm.at[cols(m)], t2_sem.at[1, lax.rem(m, 2)])
-
-        def out3():
-            return pltpu.make_async_copy(w2st.at[NT2 % 2], dwo_hbm, t2_sem.at[1, NT2 % 2])
-
         nt_in(0).start()
         loads[1].start()
         loads[0].start()
-        loads[2].start()
         pair_sum(NB - 1)
 
         @pl.loop(0, NT1)
@@ -472,10 +477,6 @@
             def _():
                 nt_in(m + 1).start()
 
-            @pl.when(m + 1 == NT1)
-            def _():
-                g_in(0).start()
-
             @pl.when(m >= 2)
             def _():
                 for cp in out1(m - 2):
@@ -502,47 +503,11 @@
         for m in (NT1 - 2, NT1 - 1):
             for cp in out1(m):
                 cp.wait()
-        loads[2].wait()
-
-        @pl.loop(0, NT2)
-        def _(m):
-            s = lax.rem(m, 2)
-            g_in(m).wait()
-
-            @pl.when(m + 1 < NT2)
-            def _():
-                g_in(m + 1).start()
-
-            @pl.when(m + 1 == NT2)
-            def _():
-                o_in().start()
-
-            @pl.when(m >= 2)
-            def _():
-                out2(m - 2).wait()
-
-            points = service_points(plan[1], NT1 + m)
-            service(points[0])
-            w2st[s, :, :D // 2] = mm_tn(nt[s], dy[:, :D // 2]).astype(BF16)
-            service(points[1])
-            w2st[s, :, D // 2:] = mm_tn(nt[s], dy[:, D // 2:]).astype(BF16)
-            out2(m).start()
-
-        o_in().wait()
-        out2(NT2 - 2).wait()
-        points = service_points(plan[1], NT1 + NT2)
-        service(points[0])
-        w2st[NT2 % 2, :, :D // 2] = mm_tn(nt[NT2 % 2], dy[:, :D // 2]).astype(BF16)
-        service(points[1])
-        w2st[NT2 % 2, :, D // 2:] = mm_tn(nt[NT2 % 2], dy[:, D // 2:]).astype(BF16)
-        out3().start()
-        out2(NT2 - 1).wait()
-        out3().wait()
 
     pl.run_scoped(
         weight_phase,
-        pltpu.VMEM((T, F), BF16), pltpu.VMEM((T, 3 * H), BF16), pltpu.VMEM((T, D), BF16), pltpu.VMEM((2, T, H), BF16),
-        pltpu.VMEM((2, H, F), BF16), pltpu.VMEM((2, H, 3 * H), BF16), pltpu.VMEM((2, H, D), BF16))
+        pltpu.VMEM((T, F), BF16), pltpu.VMEM((T, 3 * H), BF16), pltpu.VMEM((2, T, H), BF16),
+        pltpu.VMEM((2, H, F), BF16), pltpu.VMEM((2, H, 3 * H), BF16))
 
     (l3, l4, l5), last3, last4 = plan[2]
     service(([l3, l4, l5], [jnp.int32(last3), jnp.int32(last4)], [jnp.int32(0)] * 3))
@@ -579,21 +544,21 @@
             dx_fwd(t).wait_recv()
 
 
-def service_plan(blocks, tiles, keys_per_chunk):
+def service_plan(blocks, tiles):
     wire, lat, slow, count = 5.65, 2.5, 1.08, 2 * blocks
-    at, ready, now = [], [], 14.0
+    at, ready, now = [], [], 20.5
     for t in range(blocks):
-        chunks = (blocks - 1 - t) * ROWS // keys_per_chunk + 1
-        mlp = now + 3.2 * slow
-        at += [now, mlp, mlp + 0.56 * chunks * slow, mlp + 1.28 * chunks * slow]
+        keys = blocks - t
+        mlp = now + 3.6
+        at += [now, mlp, mlp + 0.4 + 0.14 * keys * slow, mlp + 0.8 + 0.32 * keys * slow]
         if t:
             ready += [mlp, mlp]
-        now = at[-1] + 2.3 * slow
+        now = at[-1] + 3.0
     ready += [now + 0.5, now + 0.5]
-    now += 2.0
+    now += 4.0
     for m in range(tiles):
-        at += [now, now + 2.1 * slow]
-        now += 4.3 * slow
+        at += [now, now + 2.3]
+        now += 5.0
     at.append(now)
     fires = []
     for step in range(3):
@@ -628,34 +593,138 @@
     return tables[0], tables[1], (tuple(done), last[0], last[1])
 
 
-def copy_kernel(*refs):
-    n = len(refs) // 4
-    pieces = []
-    for src, dst, buf, sem in zip(refs[:n], refs[n:2 * n], refs[2 * n:3 * n], refs[3 * n:]):
-        count = sem.shape[1]
-        rows = src.shape[0] // count
-        for p in range(count):
-            part = pl.ds(p * rows, rows)
-            pieces.append((pltpu.make_async_copy(src.at[part], buf.at[part], sem.at[0, p]), pltpu.make_async_copy(buf.at[part], dst.at[part], sem.at[1, p])))
-    for load, _ in pieces:
-        load.start()
-    for load, store in pieces:
+def finish_kernel(dims, dx_in, dwq_in, dw1_in, g_hbm, o_hbm, dy_hbm, dx_hbm, dwq_hbm, dw1_hbm, dw2_hbm, dwo_hbm,
+                  go, dy, wst, xbuf, wqbuf, w1buf, g_sem, y_sem, out_sem, x_sem, q_sem, u_sem):
+    T, D, F, H = dims
+    M, W = F // H + 1, min(512, D)
+    N = D // W
+    XP = 16
+    XR, UR = T // XP, D // 4
+
+    def cols(k, w):
+        return pl.ds(pl.multiple_of(k * w, w), w)
+
+    def g_in(m):
+        return pltpu.make_async_copy(g_hbm.at[:, cols(m, H)], go.at[m], g_sem.at[m])
+
+    o_in = pltpu.make_async_copy(o_hbm, go.at[M - 1], g_sem.at[M - 1])
+
+    def y_in(n):
+        return pltpu.make_async_copy(dy_hbm.at[:, cols(n, W)], dy.at[n], y_sem.at[n])
+
+    def x_copy(p):
+        return (pltpu.make_async_copy(dx_in.at[cols(p, XR)], xbuf.at[cols(p, XR)], x_sem.at[0, p]),
+                pltpu.make_async_copy(xbuf.at[cols(p, XR)], dx_hbm.at[cols(p, XR)], x_sem.at[1, p]))
+
+    def u_copy(p):
+        return (pltpu.make_async_copy(dw1_in.at[cols(p, UR)], w1buf.at[cols(p, UR)], u_sem.at[0, p]),
+                pltpu.make_async_copy(w1buf.at[cols(p, UR)], dw1_hbm.at[cols(p, UR)], u_sem.at[1, p]))
+
+    q_load = pltpu.make_async_copy(dwq_in, wqbuf, q_sem.at[0])
+    q_store = pltpu.make_async_copy(wqbuf, dwq_hbm, q_sem.at[1])
+
+    g_in(0).start()
+    y_in(0).start()
+    for m in range(1, M - 1):
+        g_in(m).start()
+    o_in.start()
+    y_in(1).start() if N > 1 else None
+    for p in range(4):
+        x_copy(p)[0].start()
+
+    def w2_out(k, m, n):
+        return pltpu.make_async_copy(wst.at[lax.rem(k, 2)], dw2_hbm.at[cols(m, H), cols(n, W)], out_sem.at[lax.rem(k, 2)])
+
+    def wo_out(k, n):
+        return pltpu.make_async_copy(wst.at[lax.rem(k, 2)], dwo_hbm.at[:, cols(n, W)], out_sem.at[lax.rem(k, 2)])
+
+    @pl.loop(0, N * M)
+    def _(k):
+        n, m = k // M, lax.rem(k, M)
+
+        @pl.when(n == 0)
+        def _():
+            pltpu.make_async_copy(o_hbm, go.at[m], g_sem.at[m]).wait()
+
+        @pl.when(m == 0)
+        def _():
+            y_in(n).wait()
+
+            @pl.when(n + 2 < N)
+            def _():
+                y_in(n + 2).start()
+
+        @pl.when(k + 4 < XP)
+        def _():
+            x_copy(k + 4)[0].start()
+
+        @pl.when((k + 4 >= XP) & (k + 4 < XP + 4))
+        def _():
+            u_copy(k + 4 - XP)[0].start()
+
+        @pl.when(k == 2)
+        def _():
+            q_load.start()
+
+        @pl.when(k == 6)
+        def _():
+            q_load.wait()
+            q_store.start()
+
+        @pl.when(k >= 2)
+        def _():
+            wo_out(k, 0).wait()
+
+        wst[lax.rem(k, 2)] = mm_tn(go[m], dy[n]).astype(BF16)
+
+        @pl.when(m < M - 1)
+        def _():
+            w2_out(k, m, n).start()
+
+        @pl.when(m == M - 1)
+        def _():
+            wo_out(k, n).start()
+
+        @pl.when(k < XP)
+        def _():
+            load, store = x_copy(k)
+            load.wait()
+            store.start()
+
+        @pl.when((k >= XP) & (k < XP + 4))
+        def _():
+            load, store = u_copy(k - XP)
+            load.wait()
+            store.start()
+
+    for k in range(N * M, XP + 4):
+        load, store = x_copy(k) if k < XP else u_copy(k - XP)
+        if k >= N * M + 4:
+            load.start()
         load.wait()
         store.start()
-    for _, store in pieces:
-        store.wait()
-
-
-def copy_out(arrays):
+    for k in (N * M - 2, N * M - 1):
+        wo_out(k, 0).wait()
+    q_store.wait()
+    for p in range(XP):
+        x_copy(p)[1].wait()
+    for p in range(4):
+        u_copy(p)[1].wait()
+
+
+def finish(dx, dwq, dw1, act, attn, dy):
+    (T, D), F, H = dx.shape, act.shape[1], attn.shape[1]
+    W = min(512, D)
     any_spec = pl.BlockSpec(memory_space=pl.ANY)
-    counts = [2 ** max(0, (a.size // (512 * 1024)).bit_length() - 1) for a in arrays]
-    size = sum(a.size * 2 for a in arrays)
     return pl.pallas_call(
-        copy_kernel, name="results",
-        out_shape=[jax.ShapeDtypeStruct(a.shape, a.dtype) for a in arrays],
-        in_specs=[any_spec] * len(arrays), out_specs=[any_spec] * len(arrays),
-        scratch_shapes=[pltpu.VMEM(a.shape, a.dtype) for a in arrays] + [pltpu.SemaphoreType.DMA((2, c)) for c in counts],
-        compiler_params=pltpu.CompilerParams(vmem_limit_bytes=size + (4 << 20)))(*arrays)
+        functools.partial(finish_kernel, (T, D, F, H)), name="finish",
+        out_shape=[jax.ShapeDtypeStruct(sh, BF16) for sh in (dx.shape, dwq.shape, dw1.shape, (F, D), (H, D))],
+        in_specs=[any_spec] * 6, out_specs=[any_spec] * 5,
+        scratch_shapes=[pltpu.VMEM((F // H + 1, T, H), BF16), pltpu.VMEM((D // W, T, W), BF16), pltpu.VMEM((2, H, W), BF16),
+                        pltpu.VMEM(dx.shape, BF16), pltpu.VMEM(dwq.shape, BF16), pltpu.VMEM(dw1.shape, BF16),
+                        pltpu.SemaphoreType.DMA((F // H + 1,)), pltpu.SemaphoreType.DMA((D // W,)), pltpu.SemaphoreType.DMA((2,)),
+                        pltpu.SemaphoreType.DMA((2, 16)), pltpu.SemaphoreType.DMA((2,)), pltpu.SemaphoreType.DMA((2, 4))],
+        compiler_params=pltpu.CompilerParams(vmem_limit_bytes=67043328))(dx, dwq, dw1, act, attn, dy)
 
 
 def rope_tables(blocks, head_dim):
@@ -678,26 +747,28 @@
         HALF = ROWS // 2
         C = min(1024, T)
         tabs = [jnp.asarray(t) for t in rope_tables(NB, H)]
+        small = jnp.concatenate([ln_mean, ln_rstd, ln_gain.astype(F32)]).reshape(2 * NB + D // ROWS, ROWS)
         any_spec = pl.BlockSpec(memory_space=pl.ANY)
         vmem = pl.BlockSpec(memory_space=pltpu.VMEM)
         sds = lambda *s: jax.ShapeDtypeStruct(s, BF16)
         outs = pl.pallas_call(
-            functools.partial(layer_kernel, (T, D, F, H, C), service_plan(NB, D // H + F // H + 1, C)),
+            functools.partial(layer_kernel, (T, D, F, H, C), service_plan(NB, D // H)),
             name="layer_backward",
-            out_shape=[sds(T, D), sds(D, 3 * H), sds(H, D), sds(D, F), sds(F, D),
+            out_shape=[sds(T, D), sds(D, 3 * H), sds(D, F),
                        sds(T, D), sds(T, F), sds(T, F), sds(T, 3 * H), sds(T, H), sds(2 * NB, HALF // 2, D), sds(2 * NB, HALF // 2, D)],
-            in_specs=[any_spec, any_spec] + [vmem] * 7 + [any_spec, any_spec, any_spec, any_spec],
-            out_specs=[any_spec] * 12,
+            in_specs=[any_spec, any_spec] + [vmem] * 5 + [any_spec, any_spec, any_spec, any_spec],
+            out_specs=[any_spec] * 10,
             scratch_shapes=[
-                pltpu.VMEM((2 * NB, HALF // 2, D), BF16), pltpu.VMEM((ROWS, D), BF16), pltpu.VMEM((2, HALF, D), BF16),
+                pltpu.VMEM((1, D), F32), pltpu.VMEM((2 * NB, HALF // 2, D), BF16), pltpu.VMEM((ROWS, D), BF16), pltpu.VMEM((2, HALF, D), BF16),
                 *[pltpu.VMEM((HALF // 2, D), BF16)] * 4,
                 pltpu.SemaphoreType.DMA((2,)), pltpu.SemaphoreType.DMA((2,))]
             + [pltpu.SemaphoreType.DMA((2 * NB,))] * 8
             + [pltpu.SemaphoreType.DMA((4,)), pltpu.SemaphoreType.DMA((2, 2)), pltpu.SemaphoreType.DMA((4,)), pltpu.SemaphoreType.DMA((4, 2)),
                pltpu.SemaphoreType.DMA((3, 2))],
             compiler_params=pltpu.CompilerParams(collective_id=0, has_side_effects=True, vmem_limit_bytes=67043328),
-        )(resid_x, grad_y, ln_gain.astype(F32).reshape(1, D), ln_mean.reshape(NB, ROWS), ln_rstd.reshape(NB, ROWS), *tabs, w_qkv, w_out.reshape(H, D), w_up, w_down)
-        grad_x, grad_w_qkv, grad_w_out, grad_w_up, grad_w_down = copy_out(outs[:5])
+        )(resid_x, grad_y, small, *tabs, w_qkv, w_out.reshape(H, D), w_up, w_down)
+        grad_x, grad_w_qkv, grad_w_up, _, act, _, _, attn, _, _ = outs
+        grad_x, grad_w_qkv, grad_w_up, grad_w_down, grad_w_out = finish(grad_x, grad_w_qkv, grad_w_up, act, attn, grad_y)
         return grad_x, grad_w_qkv, grad_w_out.reshape(1, H, D), grad_w_up, grad_w_down
 
     in_specs = (P("data", None), P("data"), P("data"), P(None), P("data", None), P(None, "model"), P("model", None, None), P(None, "model"), P("model", None))

time: 310 us -> 297 us (0.958)
  local copies, waits for them, and re-layouts: 10.1 us -> 0.63 us
  Pallas kernels: 297 us -> 293 us
    pallas_call x1, Pallas kernels: 281 us -> 260 us  [device_step(): pl.pallas_call(functools.partial(layer_kernel, (T, D, F, H, C), service_p...]
    pallas_call x1, Pallas kernels: 16 us -> 33.2 us  [finish(): pl.pallas_call(functools.partial(finish_kernel, (T, D, F, H)), name='fini...]
    unnamed x8 -> x0, local copies, waits for them, and re-layouts: 7.48 us -> none
where the time goes in v3:
time: 297 us; the launch traced here: 296 us
  Pallas kernels  293 us (99%)
    pallas_call x1, Pallas kernels, device_step(): pl.pallas_call(functools.partial(layer_kernel, (T, D, F, H, C), service_p...  260 us
    pallas_call x1, Pallas kernels, finish(): pl.pallas_call(functools.partial(finish_kernel, (T, D, F, H)), name='fini...  33.2 us

profile of v3, /device:TPU:0, one launch (start us, length us, event | category | flops | bytes accessed | tf_op | source)
XLA Modules:
  0.0 295.7 jit_solution(6319816836967299336)
XLA Ops:
  0.6 0.7 convert_element_type.3
  1.3 0.7 pad_maximum_fusion
  2.1 0.6 reshape.19.small_ref
  2.7 259.6 %layer_backward.1 = (bf16[4096,2048]{1,0:T(8,128)(2,1)}, bf16[2048,768]{1,0:T(8,128)(2,1)}, bf16[2048,1024]{1,0:T(8,128)(2,1)}, bf16[4096,2048]{1,0:T(8,128)(2,1...) custom-call(bf16[4096,2048]{1,0:T(8,128)(2,1)} %x_hbm.1, ...), custom_call_target="tpu_custom_call" | custom-call | tf_op jit(solution)/shard_map/layer_backward/pallas_call | solution.py:754
  262.3 33.2 %finish.1 = (bf16[4096,2048]{1,0:T(8,128)(2,1)}, bf16[2048,768]{1,0:T(8,128)(2,1)}, bf16[2048,1024]{1,0:T(8,128)(2,1)}, bf16[1024,2048]{1,0:T(8,128)(2,1)}, bf16[256,2048]{1,0:T(8,128)(2,1)}) custom-call(bf16[4096,2048]{1,0:T(8,128)(2,1)} %get-tuple-element.15.dx_in, bf16[2048,768]{1,0:T(8,128)(2,1)} %get-tuple-element.16.dwq_in, ...), custom_call_target="tpu_custom_call" | custom-call | tf_op jit(solution)/shard_map/finish/pallas_call | solution.py:719

commit v4 on v2

--- a/solution.py
+++ b/solution.py
@@ -30,9 +30,9 @@
     return jnp.minimum(jnp.maximum(v, 0), hi)
 
 
-def layer_kernel(dims, plan, x_hbm, dy_hbm, g_ref, mean_ref, rstd_ref, cb_ref, sb_ref, co_ref, so_ref, wqkv_hbm, wo_hbm, w1_hbm, w2_hbm,
+def layer_kernel(dims, plan, x_hbm, dy_hbm, small_ref, cb_ref, sb_ref, co_ref, so_ref, wqkv_hbm, wo_hbm, w1_hbm, w2_hbm,
                  dx_hbm, dwqkv_hbm, dwo_hbm, dw1_hbm, dw2_hbm, n_hbm, g_hbm, da_hbm, dqkv_hbm, o_hbm, zin_hbm, xin_hbm,
-                 qbuf, pst, sib_in, zst, xst, lx, ly,
+                 gain, qbuf, pst, sib_in, zst, xst, lx, ly,
                  sib_s, sib_r, qs_s, z_r, x_r, dxl_s, dxs_s, dxo_s, dxo_r, dxs_r, st_sem, in_sem, w_sem, out_sem, t2_sem):
     T, D, F, H, C = dims
     R = ROWS
@@ -51,6 +51,8 @@
     is_mid = (z == 1) | (z == 2)
     is_out = (z == 0) | (z == 3)
 
+    for c in range(D // R):
+        gain[:, c * R:(c + 1) * R] = small_ref[2 * NB + c:2 * NB + c + 1, :]
     barrier = pltpu.get_barrier_semaphore()
     pl.semaphore_signal(barrier, inc=1, device_id={"model": sibling}, device_id_type=MESH)
     pl.semaphore_signal(barrier, inc=1, device_id={"model": near}, device_id_type=MESH)
@@ -141,7 +143,7 @@
         x_copy(t).wait_send()
         mean, rstd = row_stats(NB - 1 - t // 2, core * 2 + lax.rem(t, 2))
         xh = (lx[...].astype(F32) - mean) * rstd
-        d = (qbuf[t].astype(F32) + xst[...].astype(F32)) * g_ref[...]
+        d = (qbuf[t].astype(F32) + xst[...].astype(F32)) * gain[...]
         md = jnp.sum(d, axis=1, keepdims=True) * (1.0 / D)
         mdx = jnp.sum(d * xh, axis=1, keepdims=True) * (1.0 / D)
         qbuf[t] = (ly[...].astype(F32) + rstd * (d - md - xh * mdx)).astype(BF16)
@@ -196,8 +198,8 @@
 
     def row_stats(i, part=None):
         out = []
-        for ref in (mean_ref, rstd_ref):
-            row = ref[pl.ds(i, 1), :]
+        for first in (0, NB):
+            row = small_ref[pl.ds(first + i, 1), :]
             if part is None:
                 col = jnp.broadcast_to(row, (128, R)).T
             else:
@@ -218,7 +220,7 @@
         other = jnp.where(lane < H // 8, pltpu.roll(x0, 128 - H // 8, 1), pltpu.roll(x0, H // 8, 1))
         return jnp.concatenate([x0 * cosf + other * sinf, x[:, 128:]], axis=1)
 
-    def attention_phase(kv, kT, vv, vT, dk, dv, es, dps, w1, w2, wqkv, wo, nbuf, ybuf, gst, dast, dqkvst, ost, qs, qT, do, doT, oT, dqT, msc):
+    def attention_phase(kv, kT, vv, vT, dk, dv, es, dps, w1, w2, wqkv, wo, nbuf, ybuf, gst, dast, dqkvst, ost, qs, qT, do, doT, oT, dqT, msc, stat):
         w_loads = [pltpu.make_async_copy(s, d_, w_sem.at[k]) for k, (s, d_) in enumerate(((wqkv_hbm, wqkv), (wo_hbm, wo), (w1_hbm, w1), (w2_hbm, w2)))]
 
         def blk(i):
@@ -246,7 +248,7 @@
         def normed(b):
             slot = lax.rem(b + 1, 2)
             mean, rstd = row_stats(b)
-            nbuf[slot] = (((ybuf[slot].astype(F32) - mean) * rstd) * g_ref[...]).astype(BF16)
+            nbuf[slot] = (((ybuf[slot].astype(F32) - mean) * rstd) * gain[...]).astype(BF16)
 
         def keys_values(b):
             kvp = mm(nbuf[lax.rem(b + 1, 2)], wqkv[:, H:])
@@ -342,7 +344,7 @@
             g_out.start()
             da_out.start()
 
-            @pl.when(t > 0)
+            @pl.when(t > 1)
             def _():
                 pair_sum(t - 1)
 
@@ -350,50 +352,66 @@
 
             nfull = i // QPC
 
-            def chunk(j):
-                return pl.ds(pl.multiple_of(j * C, C), C)
-
-            def pass_a(j, carry, masked):
+            below = jnp.where(lax.broadcasted_iota(jnp.int32, (R, R), 0) <= lax.broadcasted_iota(jnp.int32, (R, R), 1), 0.0, NEG)
+
+            def part(j, u, n=1):
+                return pl.ds(pl.multiple_of(j * C + u * R, R), n * R)
+
+            def pass_a(j, carry, subs, diagonal):
                 m, l, dl = carry
-                for u in range(QPC):
-                    keys = pl.ds(pl.multiple_of(j * C + u * R, R), R)
-                    st = mm(kv[keys, :], qT[...])
-                    if masked:
-                        key = j * C + u * R + lax.broadcasted_iota(jnp.int32, st.shape, 0)
-                        query = i * R + lax.broadcasted_iota(jnp.int32, st.shape, 1)
-                        st = jnp.where(key <= query, st, NEG)
-                    dp = mm(vv[keys, :], doT[...])
+                for u in range(subs):
+                    st = mm(kv[part(j, u), :], qT[...])
+                    if diagonal and u == subs - 1:
+                        st = jnp.where(below == 0.0, st, NEG)
+                    dp = mm(vv[part(j, u), :], doT[...])
                     m_new = jnp.maximum(m, jnp.max(st, axis=0, keepdims=True))
                     alpha = jnp.exp(m - m_new)
                     e = jnp.exp(st - m_new)
-                    es[keys, :] = e
-                    dps[keys, :] = dp
+                    es[part(j, u), :] = e
+                    dps[part(j, u), :] = dp
                     msc[pl.ds(j * QPC + u, 1), :] = m_new
                     m, l, dl = m_new, l * alpha + jnp.sum(e, axis=0, keepdims=True), dl * alpha + jnp.sum(e * dp, axis=0, keepdims=True)
                 return m, l, dl
 
             init = (jnp.full((1, R), NEG, F32), jnp.zeros((1, R), F32), jnp.zeros((1, R), F32))
-            carry = lax.fori_loop(0, nfull, functools.partial(pass_a, masked=False), init)
-            m, l, dl = pass_a(nfull, carry, True)
+            carry = lax.fori_loop(0, nfull, functools.partial(pass_a, subs=QPC, diagonal=False), init)
+            for row, value in enumerate(carry):
+                stat[row:row + 1, :] = value
+            for v in range(QPC):
+                @pl.when(lax.rem(i, QPC) == v)
+                def _(v=v):
+                    carry = pass_a(nfull, tuple(stat[row:row + 1, :] for row in range(3)), v + 1, True)
+                    for row, value in enumerate(carry):
+                        stat[row:row + 1, :] = value
+
             service(points[2])
-            inv_l = 1.0 / l
-            delta = dl * inv_l
+            m = stat[0:1, :]
+            inv_l = 1.0 / stat[1:2, :]
+            delta = stat[2:3, :] * inv_l
             oT[...] = jnp.zeros_like(oT)
             dqT[...] = jnp.zeros_like(dqT)
 
-            @pl.loop(0, nfull + 1)
+            def pass_b(j, subs):
+                pbs, dss = [], []
+                for u in range(subs):
+                    p = es[part(j, u), :] * (jnp.exp(msc[pl.ds(j * QPC + u, 1), :] - m) * inv_l)
+                    pbs.append(p.astype(BF16))
+                    dss.append((p * (dps[part(j, u), :] - delta)).astype(BF16))
+                pb, ds = jnp.concatenate(pbs, axis=0), jnp.concatenate(dss, axis=0)
+                keys = part(j, 0, subs)
+                oT[...] += mm(vT[:, keys], pb)
+                dqT[...] += mm(kT[:, keys], ds)
+                dv[keys, :] += mm(pb, do[...])
+                dk[keys, :] += mm(ds, qs[...])
+
+            @pl.loop(0, nfull)
             def _(j):
-                pbs, dss = [], []
-                for u in range(QPC):
-                    keys = pl.ds(pl.multiple_of(j * C + u * R, R), R)
-                    p = es[keys, :] * (jnp.exp(msc[pl.ds(j * QPC + u, 1), :] - m) * inv_l)
-                    pbs.append(p.astype(BF16))
-                    dss.append((p * (dps[keys, :] - delta)).astype(BF16))
-                pb, ds = jnp.concatenate(pbs, axis=0), jnp.concatenate(dss, axis=0)
-                oT[...] += mm(vT[:, chunk(j)], pb)
-                dqT[...] += mm(kT[:, chunk(j)], ds)
-                dv[chunk(j), :] += mm(pb, do[...])
-                dk[chunk(j), :] += mm(ds, qs[...])
+                pass_b(j, QPC)
+
+            for v in range(QPC):
+                @pl.when(lax.rem(i, QPC) == v)
+                def _(v=v):
+                    pass_b(nfull, v + 1)
 
             service(points[3])
 
@@ -414,6 +432,10 @@
             for c in range(EARLY, D, DT):
                 pst[:, c:c + DT] = (mm_nt(dast[slot], w1[c:c + DT, :]) + mm_nt(dqkvst[slot], wqkv[c:c + DT, :])).astype(BF16)
             sib_copy(t).start()
+
+            @pl.when(t == 0)
+            def _():
+                pair_sum(0)
 
         for t in (NB - 2, NB - 1):
             for cp in outs(t):
@@ -427,7 +449,7 @@
         pltpu.VMEM((2, R, D), BF16), pltpu.VMEM((2, R, D), BF16), pltpu.VMEM((2, R, F), BF16), pltpu.VMEM((2, R, F), BF16),
         pltpu.VMEM((2, R, 3 * H), BF16), pltpu.VMEM((2, R, H), BF16),
         pltpu.VMEM((R, H), BF16), pltpu.VMEM((H, R), BF16), pltpu.VMEM((R, H), BF16), pltpu.VMEM((H, R), BF16),
-        pltpu.VMEM((H, R), F32), pltpu.VMEM((H, R), F32), pltpu.VMEM((max(8, NB), R), F32))
+        pltpu.VMEM((H, R), F32), pltpu.VMEM((H, R), F32), pltpu.VMEM((max(8, NB), R), F32), pltpu.VMEM((8, R), F32))
 
     NT1, NT2 = D // H, F // H
 
@@ -579,21 +601,24 @@
             dx_fwd(t).wait_recv()
 
 
-def service_plan(blocks, tiles, keys_per_chunk):
+def service_plan(blocks, tiles):
     wire, lat, slow, count = 5.65, 2.5, 1.08, 2 * blocks
-    at, ready, now = [], [], 14.0
+    at, ready, now = [], [], 20.5
     for t in range(blocks):
-        chunks = (blocks - 1 - t) * ROWS // keys_per_chunk + 1
-        mlp = now + 3.2 * slow
-        at += [now, mlp, mlp + 0.56 * chunks * slow, mlp + 1.28 * chunks * slow]
-        if t:
+        keys = blocks - t
+        mlp = now + 3.6
+        at += [now, mlp, mlp + 0.4 + 0.14 * keys * slow, mlp + 0.8 + 0.32 * keys * slow]
+        if t > 1:
             ready += [mlp, mlp]
-        now = at[-1] + 2.3 * slow
+        now = at[-1] + 3.0
+        if t == 0:
+            now += 2.0
+            ready += [now, now]
     ready += [now + 0.5, now + 0.5]
-    now += 2.0
+    now += 4.0
     for m in range(tiles):
-        at += [now, now + 2.1 * slow]
-        now += 4.3 * slow
+        at += [now, now + 2.3]
+        now += 5.0
     at.append(now)
     fires = []
     for step in range(3):
@@ -649,13 +674,12 @@
 def copy_out(arrays):
     any_spec = pl.BlockSpec(memory_space=pl.ANY)
     counts = [2 ** max(0, (a.size // (512 * 1024)).bit_length() - 1) for a in arrays]
-    size = sum(a.size * 2 for a in arrays)
     return pl.pallas_call(
         copy_kernel, name="results",
         out_shape=[jax.ShapeDtypeStruct(a.shape, a.dtype) for a in arrays],
         in_specs=[any_spec] * len(arrays), out_specs=[any_spec] * len(arrays),
         scratch_shapes=[pltpu.VMEM(a.shape, a.dtype) for a in arrays] + [pltpu.SemaphoreType.DMA((2, c)) for c in counts],
-        compiler_params=pltpu.CompilerParams(vmem_limit_bytes=size + (4 << 20)))(*arrays)
+        compiler_params=pltpu.CompilerParams(vmem_limit_bytes=67043328))(*arrays)
 
 
 def rope_tables(blocks, head_dim):
@@ -678,25 +702,26 @@
         HALF = ROWS // 2
         C = min(1024, T)
         tabs = [jnp.asarray(t) for t in rope_tables(NB, H)]
+        small = jnp.concatenate([ln_mean, ln_rstd, ln_gain.astype(F32)]).reshape(2 * NB + D // ROWS, ROWS)
         any_spec = pl.BlockSpec(memory_space=pl.ANY)
         vmem = pl.BlockSpec(memory_space=pltpu.VMEM)
         sds = lambda *s: jax.ShapeDtypeStruct(s, BF16)
         outs = pl.pallas_call(
-            functools.partial(layer_kernel, (T, D, F, H, C), service_plan(NB, D // H + F // H + 1, C)),
+            functools.partial(layer_kernel, (T, D, F, H, C), service_plan(NB, D // H + F // H + 1)),
             name="layer_backward",
             out_shape=[sds(T, D), sds(D, 3 * H), sds(H, D), sds(D, F), sds(F, D),
                        sds(T, D), sds(T, F), sds(T, F), sds(T, 3 * H), sds(T, H), sds(2 * NB, HALF // 2, D), sds(2 * NB, HALF // 2, D)],
-            in_specs=[any_spec, any_spec] + [vmem] * 7 + [any_spec, any_spec, any_spec, any_spec],
+            in_specs=[any_spec, any_spec] + [vmem] * 5 + [any_spec, any_spec, any_spec, any_spec],
             out_specs=[any_spec] * 12,
             scratch_shapes=[
-                pltpu.VMEM((2 * NB, HALF // 2, D), BF16), pltpu.VMEM((ROWS, D), BF16), pltpu.VMEM((2, HALF, D), BF16),
+                pltpu.VMEM((1, D), F32), pltpu.VMEM((2 * NB, HALF // 2, D), BF16), pltpu.VMEM((ROWS, D), BF16), pltpu.VMEM((2, HALF, D), BF16),
                 *[pltpu.VMEM((HALF // 2, D), BF16)] * 4,
                 pltpu.SemaphoreType.DMA((2,)), pltpu.SemaphoreType.DMA((2,))]
             + [pltpu.SemaphoreType.DMA((2 * NB,))] * 8
             + [pltpu.SemaphoreType.DMA((4,)), pltpu.SemaphoreType.DMA((2, 2)), pltpu.SemaphoreType.DMA((4,)), pltpu.SemaphoreType.DMA((4, 2)),
                pltpu.SemaphoreType.DMA((3, 2))],
             compiler_params=pltpu.CompilerParams(collective_id=0, has_side_effects=True, vmem_limit_bytes=67043328),
-        )(resid_x, grad_y, ln_gain.astype(F32).reshape(1, D), ln_mean.reshape(NB, ROWS), ln_rstd.reshape(NB, ROWS), *tabs, w_qkv, w_out.reshape(H, D), w_up, w_down)
+        )(resid_x, grad_y, small, *tabs, w_qkv, w_out.reshape(H, D), w_up, w_down)
         grad_x, grad_w_qkv, grad_w_out, grad_w_up, grad_w_down = copy_out(outs[:5])
         return grad_x, grad_w_qkv, grad_w_out.reshape(1, H, D), grad_w_up, grad_w_down
 

time: 310 us -> 292 us (0.942)
  local copies, waits for them, and re-layouts: 10.1 us -> 0.63 us
  Pallas kernels: 297 us -> 288 us
    pallas_call x1, Pallas kernels: 281 us -> 269 us  [device_step(): pl.pallas_call(functools.partial(layer_kernel, (T, D, F, H, C), service_p...]
    unnamed x8 -> x0, local copies, waits for them, and re-layouts: 7.48 us -> none
where the time goes in v4:
time: 292 us; the launch traced here: 291 us
  Pallas kernels  288 us (99%)
    pallas_call x1, Pallas kernels, device_step(): pl.pallas_call(functools.partial(layer_kernel, (T, D, F, H, C), service_p...  269 us
    pallas_call x1, Pallas kernels, copy_out(): pl.pallas_call(copy_kernel, name='results', out_shape=[jax.ShapeDtypeStru...  19 us

profile of v4, /device:TPU:0, one launch (start us, length us, event | category | flops | bytes accessed | tf_op | source)
XLA Modules:
  0.0 291.1 jit_solution(9616586051078779278)
XLA Ops:
  0.6 0.7 convert_element_type.3
  1.3 0.7 pad_maximum_fusion
  2.1 0.6 reshape.19.small_ref
  2.7 269.2 %layer_backward.1 = (bf16[4096,2048]{1,0:T(8,128)(2,1)}, bf16[2048,768]{1,0:T(8,128)(2,1)}, bf16[256,2048]{1,0:T(8,128)(2,1)}, bf16[2048,1024]{1,0:T(8,128)(2,1)...) custom-call(bf16[4096,2048]{1,0:T(8,128)(2,1)} %x_hbm.1, ...), custom_call_target="tpu_custom_call" | custom-call | tf_op jit(solution)/shard_map/layer_backward/pallas_call | solution.py:709
  271.9 19.0 %results.1 = (bf16[4096,2048]{1,0:T(8,128)(2,1)}, bf16[2048,768]{1,0:T(8,128)(2,1)}, bf16[256,2048]{1,0:T(8,128)(2,1)}, bf16[2048,1024]{1,0:T(8,128)(2,1)}, bf16[1024,2048]{1,0:T(8,128)(2,1)}) custom-call(bf16[4096,2048]{1,0:T(8,128)(2,1)} %get-tuple-element.15.refs_0_, bf16[2048,768]{1,0:T(8,128)(2,1)} %get-tuple-element.16.refs_1_, ...), custom_call_target="tpu_custom_call" | custom-call | tf_op jit(solution)/shard_map/results/pallas_call | solution.py:677

commit v5 on v4

--- a/solution.py
+++ b/solution.py
@@ -615,10 +615,10 @@
             now += 2.0
             ready += [now, now]
     ready += [now + 0.5, now + 0.5]
-    now += 4.0
+    now += 5.0
     for m in range(tiles):
-        at += [now, now + 2.3]
-        now += 5.0
+        at += [now, now + 2.6]
+        now += 5.4
     at.append(now)
     fires = []
     for step in range(3):

time: 292 us -> 294 us (level)
  no operation moved by 1% of the time
where the time goes in v5:
time: 294 us; the launch traced here: 293 us
  Pallas kernels  290 us (99%)
    pallas_call x1, Pallas kernels, device_step(): pl.pallas_call(functools.partial(layer_kernel, (T, D, F, H, C), service_p...  271 us
    pallas_call x1, Pallas kernels, copy_out(): pl.pallas_call(copy_kernel, name='results', out_shape=[jax.ShapeDtypeStru...  19 us

profile of v5, /device:TPU:0, one launch (start us, length us, event | category | flops | bytes accessed | tf_op | source)
XLA Modules:
  0.0 293.1 jit_solution(14838015900956195444)
XLA Ops:
  0.6 0.7 convert_element_type.3
  1.3 0.7 pad_maximum_fusion
  2.1 0.6 reshape.19.small_ref
  2.7 271.2 %layer_backward.1 = (bf16[4096,2048]{1,0:T(8,128)(2,1)}, bf16[2048,768]{1,0:T(8,128)(2,1)}, bf16[256,2048]{1,0:T(8,128)(2,1)}, bf16[2048,1024]{1,0:T(8,128)(2,1)...) custom-call(bf16[4096,2048]{1,0:T(8,128)(2,1)} %x_hbm.1, ...), custom_call_target="tpu_custom_call" | custom-call | tf_op jit(solution)/shard_map/layer_backward/pallas_call | solution.py:709
  273.9 19.0 %results.1 = (bf16[4096,2048]{1,0:T(8,128)(2,1)}, bf16[2048,768]{1,0:T(8,128)(2,1)}, bf16[256,2048]{1,0:T(8,128)(2,1)}, bf16[2048,1024]{1,0:T(8,128)(2,1)}, bf16[1024,2048]{1,0:T(8,128)(2,1)}) custom-call(bf16[4096,2048]{1,0:T(8,128)(2,1)} %get-tuple-element.15.refs_0_, bf16[2048,768]{1,0:T(8,128)(2,1)} %get-tuple-element.16.refs_1_, ...), custom_call_target="tpu_custom_call" | custom-call | tf_op jit(solution)/shard_map/results/pallas_call | solution.py:677
